TPU v7x, 512 devices: a whole 4x8x8 slice. The times are simulated.
512 devices in a mesh: lat: 64 (over y_hi, x, z), ord: 8 (over y_lo, core).
Axes of the slice: x: 4, y: 8 (y_hi: 2, y_lo: 4; y = y_hi * 4 + y_lo), z: 8, core: 2. Of those that a mesh axis runs over, the one named last changes fastest.
Arguments:
- pressure: bfloat16 [2, 512, 5760], P(None, 'lat', 'ord'), may hold values from -6 to 6
- tables: bfloat16 [512, 512, 2048], P('ord', 'lat'), may hold values from -16 to 16
- quad_weight: float32 [512], replicated, may hold values from 0.5 to 2
- love_number: float32 [2048], replicated, may hold values from -0.5 to 0
- order_list: int32 [512], replicated, may hold values from 0 to 511, each once
- cycle_list: int32 [512], P('lat'), may hold values from 0 to 511, each once
Outputs:
- spectrum: float32 [2, 512, 2048], P(None, 'ord', 'lat')
- load_field: float32 [2, 512, 5760], P(None, 'lat', 'ord')
Inputs may be any that keep to these rules, and one draw needn't show every extreme that they name: `order_list`: every order from 0 to 511 stands in exactly one slot. `cycle_list`: every northern cycle from 0 to 511 stands in exactly one slot; the same slot of the southern half holds its mirror cycle.
All inputs are finite; a program needn't handle non-finite values.
Results may differ from a plain program's by a relative error of at most 0.0055.
Values may be sent and summed in bfloat16 or wider, within the bound.
No kernel may reach another device: no remote copies, remote signals or barrier semaphores. Data moves between devices by JAX's collectives and lax.ppermute only.
A program may use at most 64 MiB of HBM per device.

v0:
```python
import functools
import math

import jax
import jax.numpy as jnp
from jax import lax
from jax.experimental import pallas as pl
from jax.experimental.pallas import tpu as pltpu
from jax.sharding import PartitionSpec as P

NLON = 5760
DENSITY_RATIO = 3.0 * 1025.0 / 5517.0
LANES = 128
STEP = 16
F32 = jnp.float32
BF16 = jnp.bfloat16


def iota(shape, dim):
    return lax.broadcasted_iota(jnp.int32, shape, dim)


def turns(phase):
    whole = jnp.floor(phase * (1.0 / NLON))
    return (phase - whole * NLON) * (1.0 / NLON)


def cos_sin(x):
    quarter = jnp.floor(x * 4.0 + 0.5)
    y = (x - quarter * 0.25) * (2.0 * math.pi)
    z = y * y
    c = 1.0 + z * (-0.5 + z * (1 / 24 + z * (-1 / 720 + z * (1 / 40320 - z * (1 / 3628800)))))
    s = y * (1.0 + z * (-1 / 6 + z * (1 / 120 + z * (-1 / 5040 + z * (1 / 362880)))))
    q = quarter.astype(jnp.int32)
    swap = (q & 1) == 1
    cc = jnp.where(swap, s, c)
    ss = jnp.where(swap, c, s)
    cc = jnp.where(((q + 1) & 2) == 2, -cc, cc)
    ss = jnp.where((q & 2) == 2, -ss, ss)
    return cc, ss


def order_rows(o_ref, d, rows):
    half = LANES // 2
    row = jnp.broadcast_to(o_ref[pl.ds(d // 2, 1), :], (rows, LANES))
    turned = pltpu.roll(row, half, 1)
    low = iota((rows, LANES), 1) < half
    if isinstance(d, int):
        return jnp.where(low, row, turned) if d % 2 == 0 else jnp.where(low, turned, row)
    return jnp.where(low == (lax.rem(d, 2) == 0), row, turned)


def forward_kernel(o_ref, p_ref, tab_ref, part_ref):
    rows, lons = p_ref.shape
    start = (lax.axis_index("ord") * lons).astype(F32)
    spots = o_ref.shape[0] * 2
    lane = iota((STEP, LANES), 1)
    shift = jnp.where(lane >= LANES // 2, 0.75 * NLON, 0.0)
    at = iota((STEP, LANES), 0).astype(F32) + start
    group = 4
    for first in range(0, spots, group):
        carry = []
        turn = []
        for d in range(first, first + group):
            m = order_rows(o_ref, d, STEP).astype(F32)
            carry.append(cos_sin(turns(m * at + shift)))
            turn.append(cos_sin(turns(m[:8] * STEP)))
        turn = [tuple(jnp.concatenate([v, v], 0) for v in pair) for pair in turn]

        def body(t, state, first=first, turn=turn):
            base = pl.multiple_of(t * STEP, STEP)
            out = []
            for i in range(group):
                c, s = state[i]
                rc, rs = turn[i]
                col = (first + i) * LANES
                tab_ref[pl.ds(base, STEP), col : col + LANES] = c.astype(BF16)
                out.append((c * rc - s * rs, s * rc + c * rs))
            return tuple(out)

        lax.fori_loop(0, lons // STEP, body, tuple(carry), unroll=3)
    for d in range(spots):
        part_ref[d] = jnp.dot(
            p_ref[...], tab_ref[:, d * LANES : (d + 1) * LANES], preferred_element_type=F32
        )


def analysis_kernel(cyc_ref, quad_ref, r_ref, o_ref, tab_ref, x_ref):
    sources, rows, _ = r_ref.shape
    cycles = rows // 2
    half = LANES // 2
    total = r_ref[0]
    for d in range(1, sources):
        total = total + r_ref[d]
    lane8, sub8 = iota((cycles, LANES), 1), iota((cycles, LANES), 0)
    weight = jnp.zeros((cycles, LANES), F32)
    for j in range(cycles):
        weight = jnp.where(sub8 == j, quad_ref[cyc_ref[j]], weight)
    lon_scale = 1.0 / math.sqrt(NLON)
    weight = weight * (1.0 / math.sqrt(quad_ref.shape[0]))
    total = total * jnp.where(iota((rows, LANES), 1) < half, lon_scale, -lon_scale)
    north, south = total[:cycles], total[cycles:]
    folds = [(weight * (north + south)).astype(BF16), (weight * (north - south)).astype(BF16)]
    depth = tab_ref.shape[0]
    spread = (lax.rem(iota((cycles, depth), 1), cycles) == iota((cycles, depth), 0)).astype(BF16)
    own = lax.div(iota((LANES, depth), 1), cycles) == lax.rem(iota((LANES, depth), 0), half)
    wide = []
    for fold in folds:
        tiled = lax.dot_general(fold, spread, (((0,), (0,)), ((), ())), preferred_element_type=F32)
        wide.append(jnp.where(own, tiled, 0.0).astype(BF16))
    mid, quart = depth // 2, half // 2
    lhs = [
        jnp.concatenate(
            [w[c * half + k * quart : c * half + (k + 1) * quart, k * mid : (k + 1) * mid] for w in wide for c in range(2)],
            0,
        )
        for k in range(2)
    ]
    order = jnp.transpose(order_rows(o_ref, lax.axis_index("ord"), LANES).astype(F32)).astype(jnp.int32)
    degrees = tab_ref.shape[1]
    tile = 2 * LANES
    order = jnp.concatenate([order, order], 1)
    for l0 in range(0, degrees, tile):
        kept = []
        for k in range(2):
            prod = jnp.dot(lhs[k], tab_ref[k * mid : (k + 1) * mid, l0 : l0 + tile], preferred_element_type=F32)
            kept.append((prod[:half], prod[half:]))
        even = jnp.concatenate([kept[k][0][c * quart : (c + 1) * quart] for c in range(2) for k in range(2)], 0)
        odd = jnp.concatenate([kept[k][1][c * quart : (c + 1) * quart] for c in range(2) for k in range(2)], 0)
        degree = iota((LANES, tile), 1) + l0
        coeff = jnp.where(((degree + order) & 1) == 0, even, odd)
        coeff = jnp.where(degree >= order, coeff, 0.0)
        for i in range(tile // LANES):
            x_ref[l0 + i * LANES : l0 + (i + 1) * LANES, :] = jnp.transpose(
                coeff[:, i * LANES : (i + 1) * LANES]
            ).astype(BF16)


def scale_kernel(r_ref, love_ref, spec_ref, out_ref, col_ref):
    sources, share, _ = r_ref.shape
    lat = lax.axis_index("lat")
    total = r_ref[0].astype(F32)
    for d in range(1, sources):
        total = total + r_ref[d].astype(F32)
    per = LANES // share
    row = love_ref[pl.ds(lax.div(lat, per), 1), :]
    col_ref[...] = jnp.transpose(jnp.broadcast_to(row, (LANES, LANES)))
    love = col_ref[pl.ds(pl.multiple_of(lax.rem(lat, per) * share, share), share), :]
    scaled = ((DENSITY_RATIO * (1.0 + love)) * total).astype(BF16)
    for d in range(sources):
        out_ref[d] = scaled
    wide = jnp.concatenate([total] * per, 0)
    spec_ref[...] = jnp.transpose(wide)[:, :share]


def synthesis_kernel(s_ref, o_ref, tab_ref, out_ref):
    sources, rows, _ = out_ref.shape
    cycles = rows // 2
    half = LANES // 2
    depth, degrees = tab_ref.shape
    s = s_ref[...]
    odd_row = (iota((degrees, LANES), 0) & 1) == 1
    flipped = jnp.where(odd_row, -s, s)
    both = jnp.concatenate([s, flipped], 1)
    result = jnp.dot(tab_ref[...], both, preferred_element_type=F32)
    lane = lax.rem(iota((cycles, 2 * LANES), 1), half)
    picked = jnp.zeros((cycles, 2 * LANES), F32)
    for m in range(half):
        picked = jnp.where(lane == m, result[m * cycles : (m + 1) * cycles], picked)
    order = order_rows(o_ref, lax.axis_index("ord"), cycles)
    deg_scale = 1.0 / math.sqrt(degrees)
    north = picked[:, :LANES] * deg_scale
    south = jnp.where((order & 1) == 1, -picked[:, LANES:], picked[:, LANES:]) * deg_scale
    signal = jnp.concatenate([north, south], 0)
    signal = jnp.where(iota((rows, LANES), 1) < half, signal, -signal).astype(BF16)
    for d in range(sources):
        out_ref[d] = signal


def inverse_kernel(g_ref, tab_ref, out_ref):
    spots = g_ref.shape[0]
    lhs = jnp.concatenate([g_ref[d] for d in range(spots)], 1)
    field = lax.dot_general(lhs, tab_ref[...], (((1,), (1,)), ((), ())), preferred_element_type=F32)
    out_ref[...] = field * (1.0 / math.sqrt(spots * (LANES // 2)))


VM = pl.BlockSpec(memory_space=pltpu.VMEM)
SM = pl.BlockSpec(memory_space=pltpu.SMEM)


def shape(dims, kind):
    return jax.ShapeDtypeStruct(dims, kind)


def call(kernel, outs, specs, name, scratch=()):
    return pl.pallas_call(
        kernel,
        out_shape=outs,
        in_specs=specs,
        out_specs=jax.tree.map(lambda _: VM, outs),
        scratch_shapes=list(scratch),
        name=name,
    )


def swap(x, axis):
    return lax.all_to_all(x, axis, split_axis=0, concat_axis=0, tiled=True)


def per_device(pressure, tables, quad_weight, love_number, order_list, cycle_list):
    cycles, lons = pressure.shape[1:]
    own_orders, _, degrees = tables.shape
    rows = 2 * cycles
    n_ord, n_lat = lax.axis_size("ord"), lax.axis_size("lat")
    share = degrees // n_lat
    orders = order_list.reshape(-1, LANES)
    table, part = call(
        forward_kernel,
        (shape((lons, n_ord * LANES), BF16), shape((n_ord, rows, LANES), F32)),
        [VM, VM],
        "forward",
    )(orders, pressure.reshape(rows, lons))
    arrived = swap(part, "ord")
    flat = tables.reshape(own_orders * cycles, degrees)
    coeff = call(
        analysis_kernel,
        shape((degrees, LANES), BF16),
        [SM, SM, VM, VM, VM],
        "analysis",
    )(cycle_list, quad_weight, arrived, orders, flat)
    summands = swap(coeff.reshape(n_lat, share, LANES), "lat")
    spectrum, copies = call(
        scale_kernel,
        (shape((LANES, share), F32), shape((n_lat, share, LANES), BF16)),
        [VM, VM],
        "scale",
        [pltpu.VMEM((LANES, LANES), F32)],
    )(summands, love_number.reshape(-1, LANES))
    scaled = swap(copies, "lat").reshape(degrees, LANES)
    signal = call(
        synthesis_kernel,
        shape((n_ord, rows, LANES), BF16),
        [VM, VM, VM],
        "synthesis",
    )(scaled, orders, flat)
    signals = swap(signal, "ord")
    field = call(inverse_kernel, shape((rows, lons), F32), [VM, VM], "inverse")(signals, table)
    return spectrum.reshape(2, own_orders, share), field.reshape(2, cycles, lons)


def solution(mesh):
    placed = (P(None, "lat", "ord"), P("ord", "lat", None), P(), P(), P(), P("lat"))
    return jax.shard_map(
        per_device,
        mesh=mesh,
        in_specs=placed,
        out_specs=(P(None, "ord", "lat"), P(None, "lat", "ord")),
        check_vma=False,
    )
```

profile of v0, /device:TPU:1, one launch (start us, length us, event | category | flops | bytes accessed | tf_op | source)
XLA Modules:
  0.0 103.5 jit_solution(2424529619944046742)
XLA Ops:
  0.6 3.0 %forward.1 = (bf16[720,1024]{1,0:T(8,128)(2,1)}, f32[8,16,128]{2,1,0:T(8,128)}) custom-call(s32[4,128]{1,0:T(4,128)} %bitcast.15, bf16[16,720]{1,0:T(8,128)(2,1)} %bitcast.14), custom_call_target="tpu_custom_call" | custom-call | tf_op jit(solution)/shard_map/forward/pallas_call | solution.py:217
  3.6 15.8 %all_to_all.20.r_ref = f32[8,16,128]{2,1,0:T(8,128)} all-to-all(f32[8,16,128]{2,1,0:T(8,128)} %get-tuple-element.6), channel_id=1, replica_groups=mesh['lat'=64,'ord'=8] {'ord'}, dimensions={0} | all-to-all | bytes 131072 | tf_op jit(solution)/shard_map/all_to_all | solution.py:207
  19.4 3.3 %analysis.1 = bf16[2048,128]{1,0:T(8,128)(2,1)} custom-call(s32[8]{0:T(128)} %cyc_ref.1, f32[512]{0:T(512)} %quad_ref.1, f32[8,16,128]{2,1,0:T(8,128)} %all_to_all.20.r_ref, s32[4,128]{1,0:T(4,128)} %bitcast.16, bf16[512,2048]{1,0:T(8,128)(2,1)} %bitcast.8), custom_call_target="tpu_custom_call" | custom-call | tf_op jit(solution)/shard_map/analysis/pallas_call | solution.py:225
  22.7 30.4 %all_to_all.21.r_ref = bf16[64,32,128]{2,1,0:T(8,128)(2,1)} all-to-all(bf16[64,32,128]{2,1,0:T(8,128)(2,1)} %bitcast.10), channel_id=1, replica_groups=mesh['lat'=64,'ord'=8] {'lat'}, dimensions={0} | all-to-all | bytes 1048576 | tf_op jit(solution)/shard_map/all_to_all | solution.py:207
  53.1 2.0 %scale.1 = (f32[128,32]{1,0:T(8,128)}, bf16[64,32,128]{2,1,0:T(8,128)(2,1)}) custom-call(bf16[64,32,128]{2,1,0:T(8,128)(2,1)} %all_to_all.21.r_ref, f32[16,128]{1,0:T(8,128)} %bitcast.18), custom_call_target="tpu_custom_call" | custom-call | tf_op jit(solution)/shard_map/scale/pallas_call | solution.py:232
  55.1 0.0 copy-start.1
  55.1 29.7 %all_to_all.22 = bf16[64,32,128]{2,1,0:T(8,128)(2,1)} all-to-all(bf16[64,32,128]{2,1,0:T(8,128)(2,1)} %get-tuple-element.8), channel_id=1, replica_groups=mesh['lat'=64,'ord'=8] {'lat'}, dimensions={0} | all-to-all | bytes 1048576 | tf_op jit(solution)/shard_map/all_to_all | solution.py:207
  84.8 3.1 %synthesis.1 = bf16[8,16,128]{2,1,0:T(8,128)(2,1)} custom-call(bf16[2048,128]{1,0:T(8,128)(2,1)} %bitcast.11, s32[4,128]{1,0:T(4,128)} %bitcast.17, bf16[512,2048]{1,0:T(8,128)(2,1)} %bitcast.9), custom_call_target="tpu_custom_call" | custom-call | tf_op jit(solution)/shard_map/synthesis/pallas_call | solution.py:240
  88.0 7.4 %all-to-all-start.3 = ((bf16[8,16,128]{2,1,0:T(8,128)(2,1)}), bf16[8,16,128]{2,1,0:T(8,128)(2,1)S(1)}, u32[]{:S(2)}, u32[]{:S(2)}) async-start(bf16[8,16,128]{2,1,0:T(8,128)(2,1)} %synthesis.1), calls=%async_computation.3 | async-start | bytes 65536 | tf_op jit(solution)/shard_map/all_to_all | solution.py:207
  95.4 0.0 copy-done.1
  95.4 0.7 copy.8
  96.1 4.3 %all-to-all-done.3.g_ref = bf16[8,16,128]{2,1,0:T(8,128)(2,1)S(1)} async-done(((bf16[8,16,128]{2,1,0:T(8,128)(2,1)}), bf16[8,16,128]{2,1,0:T(8,128)(2,1)S(1)}, u32[]{:S(2)}, u32[]{:S(2)}) %all-to-all-start.3) | async-done | bytes 32800 | tf_op jit(solution)/shard_map/all_to_all | solution.py:207
  100.4 0.0 copy-start
  100.4 0.6 copy-done
  101.0 2.5 %inverse.1 = f32[16,720]{1,0:T(8,128)} custom-call(bf16[8,16,128]{2,1,0:T(8,128)(2,1)} %copy-done, bf16[720,1024]{1,0:T(8,128)(2,1)} %get-tuple-element.9.tab_ref), custom_call_target="tpu_custom_call" | custom-call | tf_op jit(solution)/shard_map/inverse/pallas_call | solution.py:247
Async XLA Ops:
  55.1 40.3 %copy-start.1 = (f32[128,32]{1,0:T(8,128)S(1)}, f32[128,32]{1,0:T(8,128)}, u32[]{:S(2)}) copy-start(f32[128,32]{1,0:T(8,128)} %get-tuple-element.7) | copy-start | bytes 49156
  88.0 12.4 %all-to-all-start.3 = ((bf16[8,16,128]{2,1,0:T(8,128)(2,1)}), bf16[8,16,128]{2,1,0:T(8,128)(2,1)S(1)}, u32[]{:S(2)}, u32[]{:S(2)}) async-start(bf16[8,16,128]{2,1,0:T(8,128)(2,1)} %synthesis.1), calls=%async_computation.3 | async-start | bytes 65536 | tf_op jit(solution)/shard_map/all_to_all | solution.py:207
  100.4 0.6 copy-start
where the time goes:
time: 104 us; the launch traced here: 103 us
  blocking collectives  75.9 us (73%)
  Pallas kernels  13.9 us (13%)
  starting transfers between devices  7.43 us (7%)
  waiting for transfers between devices  4.28 us (4%)
  local copies, waits for them, and re-layouts  1.29 us (1%)
    all_to_all x3, blocking collectives, swap(): return lax.all_to_all(x, axis, split_axis=0, concat_axis=0, tiled=True)  75.9 us
    all_to_all x1, starting transfers between devices, swap(): return lax.all_to_all(x, axis, split_axis=0, concat_axis=0, tiled=True)  7.43 us
    all_to_all x1, waiting for transfers between devices, swap(): return lax.all_to_all(x, axis, split_axis=0, concat_axis=0, tiled=True)  4.28 us
    pallas_call x1, Pallas kernels, per_device(): call(analysis_kernel, shape((degrees, LANES), BF16), [SM, SM, VM, VM, VM]...  3.25 us
    pallas_call x1, Pallas kernels, per_device(): call(synthesis_kernel, shape((n_ord, rows, LANES), BF16), [VM, VM, VM], '...  3.14 us
    pallas_call x1, Pallas kernels, per_device(): call(forward_kernel, (shape((lons, n_ord * LANES), BF16), shape((n_ord, r...  2.97 us
    pallas_call x1, Pallas kernels, per_device(): call(inverse_kernel, shape((rows, lons), F32), [VM, VM], 'inverse')  2.53 us
  transfers between devices with their start and end apart: 1, of which 1 were waited for; matrix products, arithmetic and copies ran while one was open for 1% of the time, Pallas kernels for 0%

commit v1 on v0

--- a/solution.py
+++ b/solution.py
@@ -50,13 +50,23 @@
     return jnp.where(low == (lax.rem(d, 2) == 0), row, turned)
 
 
-def forward_kernel(o_ref, p_ref, tab_ref, part_ref):
+def forward_kernel(
+    o_hbm, p_hbm, cyc_hbm, quad_hbm, love_hbm, t_hbm,
+    tab_ref, part_ref, own_ref, weight_ref, factor_ref, held_ref,
+    o_ref, p_ref, cyc, quad, love, col_ref, sems,
+):
+    moves = ((o_hbm, o_ref), (p_hbm, p_ref), (cyc_hbm, cyc), (quad_hbm, quad), (love_hbm, love), (t_hbm, held_ref))
+    copies = [pltpu.make_async_copy(src, dst, sems.at[i]) for i, (src, dst) in enumerate(moves)]
+    for copy in copies:
+        copy.start()
     rows, lons = p_ref.shape
     start = (lax.axis_index("ord") * lons).astype(F32)
     spots = o_ref.shape[0] * 2
     lane = iota((STEP, LANES), 1)
     shift = jnp.where(lane >= LANES // 2, 0.75 * NLON, 0.0)
     at = iota((STEP, LANES), 0).astype(F32) + start
+    copies[0].wait()
+    own_ref[...] = order_rows(o_ref, lax.axis_index("ord"), own_ref.shape[0])
     group = 4
     for first in range(0, spots, group):
         carry = []
@@ -79,25 +89,40 @@
             return tuple(out)
 
         lax.fori_loop(0, lons // STEP, body, tuple(carry), unroll=3)
+    copies[1].wait()
     for d in range(spots):
         part_ref[d] = jnp.dot(
             p_ref[...], tab_ref[:, d * LANES : (d + 1) * LANES], preferred_element_type=F32
         )
-
-
-def analysis_kernel(cyc_ref, quad_ref, r_ref, o_ref, tab_ref, x_ref):
+    cycles = cyc.shape[0]
+    share = factor_ref.shape[0]
+    lat = lax.axis_index("lat")
+    copies[4].wait()
+    per = LANES // share
+    row = love[pl.ds(lax.div(lat, per), 1), :]
+    col_ref[...] = jnp.transpose(jnp.broadcast_to(row, (LANES, LANES)))
+    factor_ref[...] = DENSITY_RATIO * (
+        1.0 + col_ref[pl.ds(pl.multiple_of(lax.rem(lat, per) * share, share), share), :]
+    )
+    copies[2].wait()
+    copies[3].wait()
+    sub = iota((cycles, LANES), 0)
+    weight = jnp.zeros((cycles, LANES), F32)
+    for j in range(cycles):
+        weight = jnp.where(sub == j, quad[cyc[j]], weight)
+    weight_ref[...] = weight * (1.0 / math.sqrt(quad.shape[0]))
+    copies[5].wait()
+
+
+def analysis_kernel(weight_ref, r_ref, own_ref, tab_ref, x_ref):
     sources, rows, _ = r_ref.shape
     cycles = rows // 2
     half = LANES // 2
     total = r_ref[0]
     for d in range(1, sources):
         total = total + r_ref[d]
-    lane8, sub8 = iota((cycles, LANES), 1), iota((cycles, LANES), 0)
-    weight = jnp.zeros((cycles, LANES), F32)
-    for j in range(cycles):
-        weight = jnp.where(sub8 == j, quad_ref[cyc_ref[j]], weight)
+    weight = weight_ref[...]
     lon_scale = 1.0 / math.sqrt(NLON)
-    weight = weight * (1.0 / math.sqrt(quad_ref.shape[0]))
     total = total * jnp.where(iota((rows, LANES), 1) < half, lon_scale, -lon_scale)
     north, south = total[:cycles], total[cycles:]
     folds = [(weight * (north + south)).astype(BF16), (weight * (north - south)).astype(BF16)]
@@ -116,7 +141,7 @@
         )
         for k in range(2)
     ]
-    order = jnp.transpose(order_rows(o_ref, lax.axis_index("ord"), LANES).astype(F32)).astype(jnp.int32)
+    order = jnp.transpose(jnp.broadcast_to(own_ref[0:1].astype(F32), (LANES, LANES))).astype(jnp.int32)
     degrees = tab_ref.shape[1]
     tile = 2 * LANES
     order = jnp.concatenate([order, order], 1)
@@ -136,24 +161,20 @@
             ).astype(BF16)
 
 
-def scale_kernel(r_ref, love_ref, spec_ref, out_ref, col_ref):
+def scale_kernel(r_ref, factor_ref, spec_ref, out_ref):
     sources, share, _ = r_ref.shape
-    lat = lax.axis_index("lat")
     total = r_ref[0].astype(F32)
     for d in range(1, sources):
         total = total + r_ref[d].astype(F32)
-    per = LANES // share
-    row = love_ref[pl.ds(lax.div(lat, per), 1), :]
-    col_ref[...] = jnp.transpose(jnp.broadcast_to(row, (LANES, LANES)))
-    love = col_ref[pl.ds(pl.multiple_of(lax.rem(lat, per) * share, share), share), :]
-    scaled = ((DENSITY_RATIO * (1.0 + love)) * total).astype(BF16)
+    scaled = (factor_ref[...] * total).astype(BF16)
     for d in range(sources):
         out_ref[d] = scaled
-    wide = jnp.concatenate([total] * per, 0)
-    spec_ref[...] = jnp.transpose(wide)[:, :share]
-
-
-def synthesis_kernel(s_ref, o_ref, tab_ref, out_ref):
+    half = LANES // 2
+    spec_ref[0] = total[:, :half]
+    spec_ref[1] = total[:, half:]
+
+
+def synthesis_kernel(s_ref, own_ref, tab_ref, out_ref):
     sources, rows, _ = out_ref.shape
     cycles = rows // 2
     half = LANES // 2
@@ -167,7 +188,7 @@
     picked = jnp.zeros((cycles, 2 * LANES), F32)
     for m in range(half):
         picked = jnp.where(lane == m, result[m * cycles : (m + 1) * cycles], picked)
-    order = order_rows(o_ref, lax.axis_index("ord"), cycles)
+    order = own_ref[0:cycles]
     deg_scale = 1.0 / math.sqrt(degrees)
     north = picked[:, :LANES] * deg_scale
     south = jnp.where((order & 1) == 1, -picked[:, LANES:], picked[:, LANES:]) * deg_scale
@@ -185,20 +206,30 @@
 
 
 VM = pl.BlockSpec(memory_space=pltpu.VMEM)
-SM = pl.BlockSpec(memory_space=pltpu.SMEM)
+HB = pl.BlockSpec(memory_space=pltpu.HBM)
 
 
 def shape(dims, kind):
-    return jax.ShapeDtypeStruct(dims, kind)
-
-
-def call(kernel, outs, specs, name, scratch=()):
+    return pltpu.VMEM(dims, kind)
+
+
+def far(x):
+    return pltpu.with_memory_space_constraint(x, pltpu.HBM)
+
+
+def near(x):
+    return pltpu.with_memory_space_constraint(x, pltpu.VMEM)
+
+
+def call(kernel, outs, specs, name, mib, flops, scratch=()):
     return pl.pallas_call(
         kernel,
         out_shape=outs,
         in_specs=specs,
-        out_specs=jax.tree.map(lambda _: VM, outs),
+        out_specs=tuple(VM for _ in outs) if isinstance(outs, tuple) else VM,
         scratch_shapes=list(scratch),
+        compiler_params=pltpu.CompilerParams(vmem_limit_bytes=mib << 20),
+        cost_estimate=pl.CostEstimate(flops=flops, bytes_accessed=1 << 20, transcendentals=0),
         name=name,
     )
 
@@ -213,39 +244,69 @@
     rows = 2 * cycles
     n_ord, n_lat = lax.axis_size("ord"), lax.axis_size("lat")
     share = degrees // n_lat
+    work = 1 << 29
     orders = order_list.reshape(-1, LANES)
-    table, part = call(
+    flat = tables.reshape(own_orders * cycles, degrees)
+    love = love_number.reshape(-1, LANES)
+    table, part, own, weight, factor, tab = call(
         forward_kernel,
-        (shape((lons, n_ord * LANES), BF16), shape((n_ord, rows, LANES), F32)),
-        [VM, VM],
+        (
+            shape((lons, n_ord * LANES), BF16),
+            shape((n_ord, rows, LANES), F32),
+            shape((8, LANES), jnp.int32),
+            shape((cycles, LANES), F32),
+            shape((share, LANES), F32),
+            shape(flat.shape, BF16),
+        ),
+        [HB] * 6,
         "forward",
-    )(orders, pressure.reshape(rows, lons))
+        8,
+        work,
+        [
+            pltpu.VMEM(orders.shape, jnp.int32),
+            pltpu.VMEM((rows, lons), BF16),
+            pltpu.SMEM(cycle_list.shape, jnp.int32),
+            pltpu.SMEM(quad_weight.shape, F32),
+            pltpu.VMEM(love.shape, F32),
+            pltpu.VMEM((LANES, LANES), F32),
+            pltpu.SemaphoreType.DMA((6,)),
+        ],
+    )(far(orders), far(pressure.reshape(rows, lons)), far(cycle_list), far(quad_weight), far(love), far(flat))
     arrived = swap(part, "ord")
-    flat = tables.reshape(own_orders * cycles, degrees)
     coeff = call(
         analysis_kernel,
         shape((degrees, LANES), BF16),
-        [SM, SM, VM, VM, VM],
+        [VM, VM, VM, VM],
         "analysis",
-    )(cycle_list, quad_weight, arrived, orders, flat)
+        6,
+        work,
+    )(near(weight), near(arrived), near(own), near(tab))
     summands = swap(coeff.reshape(n_lat, share, LANES), "lat")
     spectrum, copies = call(
         scale_kernel,
-        (shape((LANES, share), F32), shape((n_lat, share, LANES), BF16)),
+        (
+            jax.ShapeDtypeStruct((2, share, own_orders), F32),
+            shape((n_lat, share, LANES), BF16),
+        ),
         [VM, VM],
         "scale",
-        [pltpu.VMEM((LANES, LANES), F32)],
-    )(summands, love_number.reshape(-1, LANES))
+        4,
+        work,
+    )(near(summands), near(factor))
     scaled = swap(copies, "lat").reshape(degrees, LANES)
     signal = call(
         synthesis_kernel,
         shape((n_ord, rows, LANES), BF16),
         [VM, VM, VM],
         "synthesis",
-    )(scaled, orders, flat)
+        8,
+        work,
+    )(near(scaled), near(own), near(tab))
     signals = swap(signal, "ord")
-    field = call(inverse_kernel, shape((rows, lons), F32), [VM, VM], "inverse")(signals, table)
-    return spectrum.reshape(2, own_orders, share), field.reshape(2, cycles, lons)
+    field = call(inverse_kernel, jax.ShapeDtypeStruct((rows, lons), F32), [VM, VM], "inverse", 6, work)(
+        near(signals), near(table)
+    )
+    return jnp.transpose(spectrum, (0, 2, 1)), field.reshape(2, cycles, lons)
 
 
 def solution(mesh):

time: 104 us -> 92.4 us (0.89)
  blocking collectives: 75.9 us -> 85.7 us
  Pallas kernels: 13.9 us -> 5.77 us
  starting transfers between devices: 7.43 us -> 0 us
  waiting for transfers between devices: 4.28 us -> 0 us
  local copies, waits for them, and re-layouts: 1.29 us -> 0 us
    all_to_all x3 -> x4, blocking collectives: 75.9 us -> 85.7 us  [swap(): return lax.all_to_all(x, axis, split_axis=0, concat_axis=0, tiled=True)]
    all_to_all x1 -> x0, starting transfers between devices: 7.43 us -> none  [swap(): return lax.all_to_all(x, axis, split_axis=0, concat_axis=0, tiled=True)]
    pallas_call x3, Pallas kernels: 7.79 us -> 2.71 us  [the longest x1 1.13 us: per_device(): call(inverse_kernel, jax.ShapeDtypeStruct((rows, lons), F32), [VM, VM], '...]
    all_to_all x1 -> x0, waiting for transfers between devices: 4.28 us -> none  [swap(): return lax.all_to_all(x, axis, split_axis=0, concat_axis=0, tiled=True)]
    pallas_call x1, Pallas kernels: 3.14 us -> 0.74 us  [per_device(): call(synthesis_kernel, shape((n_ord, rows, LANES), BF16), [VM, VM, VM], '...]
    unnamed x5 -> x0, local copies, waits for them, and re-layouts: 1.29 us -> none
  transfers between devices with their start and end apart: 1 -> 0, of which waited for: 1 -> 0; matrix products, arithmetic and copies ran while one was open for 1% -> 0% of each run, Pallas kernels for 0% -> 0%
where the time goes in v1:
time: 92.4 us; the launch traced here: 92.1 us
  blocking collectives  85.7 us (93%)
  Pallas kernels  5.77 us (6%)
    all_to_all x4, blocking collectives, swap(): return lax.all_to_all(x, axis, split_axis=0, concat_axis=0, tiled=True)  85.7 us
    pallas_call x1, Pallas kernels, per_device(): call(forward_kernel, (shape((lons, n_ord * LANES), BF16), shape((n_ord, r...  2.32 us

profile of v1, /device:TPU:1, one launch (start us, length us, event | category | flops | bytes accessed | tf_op | source)
XLA Modules:
  0.0 92.1 jit_solution(15330349206632448645)
XLA Ops:
  0.6 2.3 %forward.1 = (bf16[720,1024]{1,0:T(8,128)(2,1)S(1)}, f32[8,16,128]{2,1,0:T(8,128)S(1)}, s32[8,128]{1,0:T(8,128)S(1)}, f32[8,128]{1,0:T(8,128)S(1)}, f32[32,128]{...) custom-call(s32[4,128]{1,0:T(4,128)} %bitcast.13, bf16[16,720]{1,0:T(8,128)(2,1)} %bitcast.11, s32[8]{0:T(128)} %cyc_hbm.1, ...), custom_call_target="tpu_custom_call" | custom-call | flops 536870912 | bytes 1048576 | tf_op jit(solution)/shard_map/forward/pallas_call | solution.py:251
  3.0 14.3 %all_to_all.20.r_ref = f32[8,16,128]{2,1,0:T(8,128)S(1)} all-to-all(f32[8,16,128]{2,1,0:T(8,128)S(1)} %get-tuple-element.11), channel_id=1, replica_groups=mesh['lat'=64,'ord'=8] {'ord'}, dimensions={0} | all-to-all | bytes 131072 | tf_op jit(solution)/shard_map/all_to_all | solution.py:238
  17.2 0.8 analysis.1
  18.0 30.1 %all_to_all.21.r_ref = bf16[64,32,128]{2,1,0:T(8,128)(2,1)S(1)} all-to-all(bf16[64,32,128]{2,1,0:T(8,128)(2,1)S(1)} %bitcast.9), channel_id=1, replica_groups=mesh['lat'=64,'ord'=8] {'lat'}, dimensions={0} | all-to-all | bytes 1048576 | tf_op jit(solution)/shard_map/all_to_all | solution.py:238
  48.1 0.8 scale.1
  48.9 29.0 %all_to_all.22 = bf16[64,32,128]{2,1,0:T(8,128)(2,1)S(1)} all-to-all(bf16[64,32,128]{2,1,0:T(8,128)(2,1)S(1)} %get-tuple-element.16), channel_id=1, replica_groups=mesh['lat'=64,'ord'=8] {'lat'}, dimensions={0} | all-to-all | bytes 1048576 | tf_op jit(solution)/shard_map/all_to_all | solution.py:238
  77.8 0.7 synthesis.1
  78.6 12.4 %all_to_all.23.g_ref = bf16[8,16,128]{2,1,0:T(8,128)(2,1)S(1)} all-to-all(bf16[8,16,128]{2,1,0:T(8,128)(2,1)S(1)} %synthesis.1), channel_id=1, replica_groups=mesh['lat'=64,'ord'=8] {'ord'}, dimensions={0} | all-to-all | bytes 65536 | tf_op jit(solution)/shard_map/all_to_all | solution.py:238
  91.0 1.1 %inverse.1 = f32[16,720]{1,0:T(8,128)} custom-call(bf16[8,16,128]{2,1,0:T(8,128)(2,1)S(1)} %all_to_all.23.g_ref, bf16[720,1024]{1,0:T(8,128)(2,1)S(1)} %get-tuple-element.17.tab_ref), custom_call_target="tpu_custom_call" | custom-call | flops 536870912 | bytes 1048576 | tf_op jit(solution)/shard_map/inverse/pallas_call | solution.py:306

commit v2 on v1

--- a/solution.py
+++ b/solution.py
@@ -6,18 +6,30 @@
 from jax import lax
 from jax.experimental import pallas as pl
 from jax.experimental.pallas import tpu as pltpu
+from jax.sharding import Mesh
 from jax.sharding import PartitionSpec as P
 
 NLON = 5760
 DENSITY_RATIO = 3.0 * 1025.0 / 5517.0
 LANES = 128
 STEP = 16
+FAR, SIDE, RUN = 2, 4, 8
+LAT = ("yh", "x", "z")
 F32 = jnp.float32
 BF16 = jnp.bfloat16
 
 
 def iota(shape, dim):
     return lax.broadcasted_iota(jnp.int32, shape, dim)
+
+
+def lat_index(far):
+    return (far * SIDE + lax.axis_index("x")) * RUN + lax.axis_index("z")
+
+
+def place(lat):
+    far, side, run = lat // (SIDE * RUN), lat // RUN % SIDE, lat % RUN
+    return (side * RUN + run) * FAR + far
 
 
 def turns(phase):
@@ -95,15 +107,16 @@
             p_ref[...], tab_ref[:, d * LANES : (d + 1) * LANES], preferred_element_type=F32
         )
     cycles = cyc.shape[0]
-    share = factor_ref.shape[0]
-    lat = lax.axis_index("lat")
+    share = factor_ref.shape[0] // FAR
     copies[4].wait()
     per = LANES // share
-    row = love[pl.ds(lax.div(lat, per), 1), :]
-    col_ref[...] = jnp.transpose(jnp.broadcast_to(row, (LANES, LANES)))
-    factor_ref[...] = DENSITY_RATIO * (
-        1.0 + col_ref[pl.ds(pl.multiple_of(lax.rem(lat, per) * share, share), share), :]
-    )
+    for far_at in range(FAR):
+        lat = lat_index(far_at)
+        row = love[pl.ds(lax.div(lat, per), 1), :]
+        col_ref[far_at] = jnp.transpose(jnp.broadcast_to(row, (LANES, LANES)))
+        factor_ref[far_at * share : (far_at + 1) * share] = DENSITY_RATIO * (
+            1.0 + col_ref[far_at, pl.ds(pl.multiple_of(lax.rem(lat, per) * share, share), share), :]
+        )
     copies[2].wait()
     copies[3].wait()
     sub = iota((cycles, LANES), 0)
@@ -143,6 +156,7 @@
     ]
     order = jnp.transpose(jnp.broadcast_to(own_ref[0:1].astype(F32), (LANES, LANES))).astype(jnp.int32)
     degrees = tab_ref.shape[1]
+    share = degrees // (FAR * SIDE * RUN)
     tile = 2 * LANES
     order = jnp.concatenate([order, order], 1)
     for l0 in range(0, degrees, tile):
@@ -156,22 +170,42 @@
         coeff = jnp.where(((degree + order) & 1) == 0, even, odd)
         coeff = jnp.where(degree >= order, coeff, 0.0)
         for i in range(tile // LANES):
-            x_ref[l0 + i * LANES : l0 + (i + 1) * LANES, :] = jnp.transpose(
-                coeff[:, i * LANES : (i + 1) * LANES]
-            ).astype(BF16)
+            turned = jnp.transpose(coeff[:, i * LANES : (i + 1) * LANES]).astype(BF16)
+            for b in range(LANES // share):
+                at = place((l0 + i * LANES) // share + b) * share
+                x_ref[at : at + share, :] = turned[b * share : (b + 1) * share]
+
+
+def added(r_ref):
+    total = r_ref[0].astype(F32)
+    for d in range(1, r_ref.shape[0]):
+        total = total + r_ref[d].astype(F32)
+    return total
+
+
+def side_kernel(r_ref, out_ref):
+    total = added(r_ref).astype(BF16)
+    for d in range(out_ref.shape[0]):
+        out_ref[d] = total
 
 
 def scale_kernel(r_ref, factor_ref, spec_ref, out_ref):
-    sources, share, _ = r_ref.shape
-    total = r_ref[0].astype(F32)
-    for d in range(1, sources):
-        total = total + r_ref[d].astype(F32)
+    total = added(r_ref)
     scaled = (factor_ref[...] * total).astype(BF16)
-    for d in range(sources):
+    for d in range(out_ref.shape[0]):
         out_ref[d] = scaled
     half = LANES // 2
-    spec_ref[0] = total[:, :half]
-    spec_ref[1] = total[:, half:]
+    share = spec_ref.shape[1]
+    own = total[:share]
+    for far_at in range(1, FAR):
+        own = jnp.where(lax.axis_index("yh") == far_at, total[far_at * share : (far_at + 1) * share], own)
+    spec_ref[0] = own[:, :half]
+    spec_ref[1] = own[:, half:]
+
+
+def spread_kernel(s_ref, out_ref):
+    for d in range(out_ref.shape[0]):
+        out_ref[d] = s_ref[...]
 
 
 def synthesis_kernel(s_ref, own_ref, tab_ref, out_ref):
@@ -179,7 +213,9 @@
     cycles = rows // 2
     half = LANES // 2
     depth, degrees = tab_ref.shape
-    s = s_ref[...]
+    blocks = FAR * SIDE * RUN
+    share = degrees // blocks
+    s = jnp.concatenate([s_ref[place(b) * share : (place(b) + 1) * share, :] for b in range(blocks)], 0)
     odd_row = (iota((degrees, LANES), 0) & 1) == 1
     flipped = jnp.where(odd_row, -s, s)
     both = jnp.concatenate([s, flipped], 1)
@@ -242,8 +278,8 @@
     cycles, lons = pressure.shape[1:]
     own_orders, _, degrees = tables.shape
     rows = 2 * cycles
-    n_ord, n_lat = lax.axis_size("ord"), lax.axis_size("lat")
-    share = degrees // n_lat
+    n_ord = lax.axis_size("ord")
+    share = degrees // (FAR * SIDE * RUN)
     work = 1 << 29
     orders = order_list.reshape(-1, LANES)
     flat = tables.reshape(own_orders * cycles, degrees)
@@ -255,7 +291,7 @@
             shape((n_ord, rows, LANES), F32),
             shape((8, LANES), jnp.int32),
             shape((cycles, LANES), F32),
-            shape((share, LANES), F32),
+            shape((FAR * share, LANES), F32),
             shape(flat.shape, BF16),
         ),
         [HB] * 6,
@@ -268,7 +304,7 @@
             pltpu.SMEM(cycle_list.shape, jnp.int32),
             pltpu.SMEM(quad_weight.shape, F32),
             pltpu.VMEM(love.shape, F32),
-            pltpu.VMEM((LANES, LANES), F32),
+            pltpu.VMEM((FAR, LANES, LANES), F32),
             pltpu.SemaphoreType.DMA((6,)),
         ],
     )(far(orders), far(pressure.reshape(rows, lons)), far(cycle_list), far(quad_weight), far(love), far(flat))
@@ -281,19 +317,25 @@
         6,
         work,
     )(near(weight), near(arrived), near(own), near(tab))
-    summands = swap(coeff.reshape(n_lat, share, LANES), "lat")
+    block = FAR * share
+    wide = RUN * block
+    sides = swap(coeff.reshape(SIDE, wide, LANES), "x")
+    partial = call(side_kernel, shape((FAR, wide, LANES), BF16), [VM], "side", 4, work)(near(sides))
+    summands = swap(partial.reshape(FAR * RUN, block, LANES), ("yh", "z"))
     spectrum, copies = call(
         scale_kernel,
         (
             jax.ShapeDtypeStruct((2, share, own_orders), F32),
-            shape((n_lat, share, LANES), BF16),
+            shape((RUN, block, LANES), BF16),
         ),
         [VM, VM],
         "scale",
         4,
         work,
     )(near(summands), near(factor))
-    scaled = swap(copies, "lat").reshape(degrees, LANES)
+    runs = swap(copies, "z").reshape(wide, LANES)
+    again = call(spread_kernel, shape((SIDE, wide, LANES), BF16), [VM], "spread", 4, work)(near(runs))
+    scaled = swap(again, "x").reshape(degrees, LANES)
     signal = call(
         synthesis_kernel,
         shape((n_ord, rows, LANES), BF16),
@@ -310,11 +352,12 @@
 
 
 def solution(mesh):
-    placed = (P(None, "lat", "ord"), P("ord", "lat", None), P(), P(), P(), P("lat"))
+    split = Mesh(mesh.devices.reshape(FAR, SIDE, RUN, -1), (*LAT, "ord"))
+    placed = (P(None, LAT, "ord"), P("ord", LAT, None), P(), P(), P(), P(LAT))
     return jax.shard_map(
         per_device,
-        mesh=mesh,
+        mesh=split,
         in_specs=placed,
-        out_specs=(P(None, "ord", "lat"), P(None, "lat", "ord")),
+        out_specs=(P(None, "ord", LAT), P(None, LAT, "ord")),
         check_vma=False,
     )

time: 92.4 us -> 89.3 us (0.966)
  blocking collectives: 85.7 us -> 82.4 us
    all_to_all x4 -> x6, blocking collectives: 85.7 us -> 82.4 us  [swap(): return lax.all_to_all(x, axis, split_axis=0, concat_axis=0, tiled=True)]
where the time goes in v2:
time: 89.3 us; the launch traced here: 88.9 us
  blocking collectives  82.4 us (92%)
  Pallas kernels  5.88 us (7%)
    all_to_all x6, blocking collectives, swap(): return lax.all_to_all(x, axis, split_axis=0, concat_axis=0, tiled=True)  82.4 us
    pallas_call x1, Pallas kernels, per_device(): call(forward_kernel, (shape((lons, n_ord * LANES), BF16), shape((n_ord, r...  2.32 us

profile of v2, /device:TPU:1, one launch (start us, length us, event | category | flops | bytes accessed | tf_op | source)
XLA Modules:
  0.0 88.9 jit_solution(9042906296690281545)
XLA Ops:
  0.6 2.3 %forward.1 = (bf16[720,1024]{1,0:T(8,128)(2,1)S(1)}, f32[8,16,128]{2,1,0:T(8,128)S(1)}, s32[8,128]{1,0:T(8,128)S(1)}, f32[8,128]{1,0:T(8,128)S(1)}, f32[64,128]{...) custom-call(s32[4,128]{1,0:T(4,128)} %bitcast.17, bf16[16,720]{1,0:T(8,128)(2,1)} %bitcast.15, s32[8]{0:T(128)} %cyc_hbm.1, ...), custom_call_target="tpu_custom_call" | custom-call | flops 536870912 | bytes 1048576 | tf_op jit(solution)/shard_map/forward/pallas_call | solution.py:287
  3.0 14.3 %all_to_all.30.r_ref = f32[8,16,128]{2,1,0:T(8,128)S(1)} all-to-all(f32[8,16,128]{2,1,0:T(8,128)S(1)} %get-tuple-element.11), channel_id=1, replica_groups=mesh['yh'=2,'x'=4,'z'=8,'ord'=8] {'ord'}, dimensions={0} | all-to-all | bytes 131072 | tf_op jit(solution)/shard_map/all_to_all | solution.py:274
  17.2 0.8 analysis.1
  18.1 10.9 %all_to_all.31.r_ref = bf16[4,512,128]{2,1,0:T(8,128)(2,1)S(1)} all-to-all(bf16[4,512,128]{2,1,0:T(8,128)(2,1)S(1)} %bitcast.11), channel_id=1, replica_groups=mesh['yh'=2,'x'=4,'z'=8,'ord'=8] {'x'}, dimensions={0} | all-to-all | bytes 1048576 | tf_op jit(solution)/shard_map/all_to_all | solution.py:274
  29.0 0.1 side.1
  29.1 22.6 %all_to_all.32.r_ref = bf16[16,64,128]{2,1,0:T(8,128)(2,1)S(1)} all-to-all(bf16[16,64,128]{2,1,0:T(8,128)(2,1)S(1)} %bitcast.12), channel_id=1, replica_groups=mesh['yh'=2,'x'=4,'z'=8,'ord'=8] {'yh','z'}, dimensions={0} | all-to-all | bytes 524288 | tf_op jit(solution)/shard_map/all_to_all | solution.py:274
  51.6 0.7 scale.1
  52.4 10.9 %all_to_all.33 = bf16[8,64,128]{2,1,0:T(8,128)(2,1)S(1)} all-to-all(bf16[8,64,128]{2,1,0:T(8,128)(2,1)S(1)} %get-tuple-element.16), channel_id=1, replica_groups=mesh['yh'=2,'x'=4,'z'=8,'ord'=8] {'z'}, dimensions={0} | all-to-all | bytes 262144 | tf_op jit(solution)/shard_map/all_to_all | solution.py:274
  63.2 0.1 spread.1
  63.3 9.3 %all_to_all.34 = bf16[4,512,128]{2,1,0:T(8,128)(2,1)S(1)} all-to-all(bf16[4,512,128]{2,1,0:T(8,128)(2,1)S(1)} %spread.1), channel_id=1, replica_groups=mesh['yh'=2,'x'=4,'z'=8,'ord'=8] {'x'}, dimensions={0} | all-to-all | bytes 1048576 | tf_op jit(solution)/shard_map/all_to_all | solution.py:274
  72.7 0.7 synthesis.1
  73.4 14.4 %all_to_all.35.g_ref = bf16[8,16,128]{2,1,0:T(8,128)(2,1)S(1)} all-to-all(bf16[8,16,128]{2,1,0:T(8,128)(2,1)S(1)} %synthesis.1), channel_id=1, replica_groups=mesh['yh'=2,'x'=4,'z'=8,'ord'=8] {'ord'}, dimensions={0} | all-to-all | bytes 65536 | tf_op jit(solution)/shard_map/all_to_all | solution.py:274
  87.8 1.1 %inverse.1 = f32[16,720]{1,0:T(8,128)} custom-call(bf16[8,16,128]{2,1,0:T(8,128)(2,1)S(1)} %all_to_all.35.g_ref, bf16[720,1024]{1,0:T(8,128)(2,1)S(1)} %get-tuple-element.17.tab_ref), custom_call_target="tpu_custom_call" | custom-call | flops 536870912 | bytes 1048576 | tf_op jit(solution)/shard_map/inverse/pallas_call | solution.py:348

commit v3 on v2

--- a/solution.py
+++ b/solution.py
@@ -15,6 +15,10 @@
 STEP = 16
 FAR, SIDE, RUN = 2, 4, 8
 LAT = ("yh", "x", "z")
+SIDES = [2, 3, 0, 1]
+RUNS = [4, 5, 6, 7, 0, 1, 2, 3]
+SPOTS = [7, 6, 5, 4, 3, 2, 1, 0]
+MEMBERS = {"x": SIDES, "z": RUNS, "ord": SPOTS, ("yh", "z"): [RUN + z for z in RUNS] + RUNS}
 F32 = jnp.float32
 BF16 = jnp.bfloat16
 
@@ -29,7 +33,7 @@
 
 def place(lat):
     far, side, run = lat // (SIDE * RUN), lat // RUN % SIDE, lat % RUN
-    return (side * RUN + run) * FAR + far
+    return (SIDES.index(side) * RUN + RUNS.index(run)) * FAR + far
 
 
 def turns(phase):
@@ -103,7 +107,7 @@
         lax.fori_loop(0, lons // STEP, body, tuple(carry), unroll=3)
     copies[1].wait()
     for d in range(spots):
-        part_ref[d] = jnp.dot(
+        part_ref[SPOTS.index(d)] = jnp.dot(
             p_ref[...], tab_ref[:, d * LANES : (d + 1) * LANES], preferred_element_type=F32
         )
     cycles = cyc.shape[0]
@@ -236,7 +240,7 @@
 
 def inverse_kernel(g_ref, tab_ref, out_ref):
     spots = g_ref.shape[0]
-    lhs = jnp.concatenate([g_ref[d] for d in range(spots)], 1)
+    lhs = jnp.concatenate([g_ref[SPOTS.index(d)] for d in range(spots)], 1)
     field = lax.dot_general(lhs, tab_ref[...], (((1,), (1,)), ((), ())), preferred_element_type=F32)
     out_ref[...] = field * (1.0 / math.sqrt(spots * (LANES // 2)))
 
@@ -271,7 +275,9 @@
 
 
 def swap(x, axis):
-    return lax.all_to_all(x, axis, split_axis=0, concat_axis=0, tiled=True)
+    return lax.all_to_all(
+        x, axis, split_axis=0, concat_axis=0, axis_index_groups=[MEMBERS[axis]], tiled=True
+    )
 
 
 def per_device(pressure, tables, quad_weight, love_number, order_list, cycle_list):

time: 89.3 us -> 82.3 us (0.922)
  blocking collectives: 82.4 us -> 74.8 us
    all_to_all x6, blocking collectives: 82.4 us -> 74.8 us  [swap(): lax.all_to_all(x, axis, split_axis=0, concat_axis=0, axis_index_groups=[M...]
where the time goes in v3:
time: 82.3 us; the launch traced here: 81.4 us
  blocking collectives  74.8 us (91%)
  Pallas kernels  5.85 us (7%)
    all_to_all x6, blocking collectives, swap(): lax.all_to_all(x, axis, split_axis=0, concat_axis=0, axis_index_groups=[M...  74.8 us
    pallas_call x1, Pallas kernels, per_device(): call(forward_kernel, (shape((lons, n_ord * LANES), BF16), shape((n_ord, r...  2.32 us

profile of v3, /device:TPU:1, one launch (start us, length us, event | category | flops | bytes accessed | tf_op | source)
XLA Modules:
  0.0 81.4 jit_solution(14786957828023499073)
XLA Ops:
  0.6 2.3 %forward.1 = (bf16[720,1024]{1,0:T(8,128)(2,1)S(1)}, f32[8,16,128]{2,1,0:T(8,128)S(1)}, s32[8,128]{1,0:T(8,128)S(1)}, f32[8,128]{1,0:T(8,128)S(1)}, f32[64,128]{...) custom-call(s32[4,128]{1,0:T(4,128)} %bitcast.17, bf16[16,720]{1,0:T(8,128)(2,1)} %bitcast.15, s32[8]{0:T(128)} %cyc_hbm.1, ...), custom_call_target="tpu_custom_call" | custom-call | flops 536870912 | bytes 1048576 | tf_op jit(solution)/shard_map/forward/pallas_call | solution.py:293
  3.0 13.8 %all_to_all.30.r_ref = f32[8,16,128]{2,1,0:T(8,128)S(1)} all-to-all(f32[8,16,128]{2,1,0:T(8,128)S(1)} %get-tuple-element.11), channel_id=1, replica_groups={{7,6,5,4,3,2,1,0},{15,14,13,12,11,10,9,8},{23,22,21,20,19,18,17,16},{31..., dimensions={0} | all-to-all | bytes 131072 | tf_op jit(solution)/shard_map/all_to_all | solution.py:278
  16.8 0.8 analysis.1
  17.6 10.1 %all_to_all.31.r_ref = bf16[4,512,128]{2,1,0:T(8,128)(2,1)S(1)} all-to-all(bf16[4,512,128]{2,1,0:T(8,128)(2,1)S(1)} %bitcast.11), channel_id=1, replica_groups={{128,192,0,64},{129,193,1,65},{130,194,2,66},{131,195,3,67},{132,196,4,..., dimensions={0} | all-to-all | bytes 1048576 | tf_op jit(solution)/shard_map/all_to_all | solution.py:278
  27.7 0.1 side.1
  27.7 21.1 %all_to_all.32.r_ref = bf16[16,64,128]{2,1,0:T(8,128)(2,1)S(1)} all-to-all(bf16[16,64,128]{2,1,0:T(8,128)(2,1)S(1)} %bitcast.12), channel_id=1, replica_groups={{288,296,304,312,256,264,272,280,32,40,48,56,0,8,16,24},{289,297,305,31..., dimensions={0} | all-to-all | bytes 524288 | tf_op jit(solution)/shard_map/all_to_all | solution.py:278
  48.8 0.7 scale.1
  49.6 9.5 %all_to_all.33 = bf16[8,64,128]{2,1,0:T(8,128)(2,1)S(1)} all-to-all(bf16[8,64,128]{2,1,0:T(8,128)(2,1)S(1)} %get-tuple-element.16), channel_id=1, replica_groups={{32,40,48,56,0,8,16,24},{33,41,49,57,1,9,17,25},{34,42,50,58,2,10,18,26..., dimensions={0} | all-to-all | bytes 262144 | tf_op jit(solution)/shard_map/all_to_all | solution.py:278
  59.0 0.1 spread.1
  59.1 10.0 %all_to_all.34 = bf16[4,512,128]{2,1,0:T(8,128)(2,1)S(1)} all-to-all(bf16[4,512,128]{2,1,0:T(8,128)(2,1)S(1)} %spread.1), channel_id=1, replica_groups={{128,192,0,64},{129,193,1,65},{130,194,2,66},{131,195,3,67},{132,196,4,..., dimensions={0} | all-to-all | bytes 1048576 | tf_op jit(solution)/shard_map/all_to_all | solution.py:278
  69.1 0.7 synthesis.1
  69.8 10.4 %all_to_all.35.g_ref = bf16[8,16,128]{2,1,0:T(8,128)(2,1)S(1)} all-to-all(bf16[8,16,128]{2,1,0:T(8,128)(2,1)S(1)} %synthesis.1), channel_id=1, replica_groups={{7,6,5,4,3,2,1,0},{15,14,13,12,11,10,9,8},{23,22,21,20,19,18,17,16},{31..., dimensions={0} | all-to-all | bytes 65536 | tf_op jit(solution)/shard_map/all_to_all | solution.py:278
  80.2 1.1 %inverse.1 = f32[16,720]{1,0:T(8,128)} custom-call(bf16[8,16,128]{2,1,0:T(8,128)(2,1)S(1)} %all_to_all.35.g_ref, bf16[720,1024]{1,0:T(8,128)(2,1)S(1)} %get-tuple-element.17.tab_ref), custom_call_target="tpu_custom_call" | custom-call | flops 536870912 | bytes 1048576 | tf_op jit(solution)/shard_map/inverse/pallas_call | solution.py:354

commit v4 on v3

--- a/solution.py
+++ b/solution.py
@@ -81,7 +81,8 @@
     lane = iota((STEP, LANES), 1)
     shift = jnp.where(lane >= LANES // 2, 0.75 * NLON, 0.0)
     at = iota((STEP, LANES), 0).astype(F32) + start
-    copies[0].wait()
+    for copy in copies[:5]:
+        copy.wait()
     own_ref[...] = order_rows(o_ref, lax.axis_index("ord"), own_ref.shape[0])
     group = 4
     for first in range(0, spots, group):
@@ -89,30 +90,28 @@
         turn = []
         for d in range(first, first + group):
             m = order_rows(o_ref, d, STEP).astype(F32)
-            carry.append(cos_sin(turns(m * at + shift)))
-            turn.append(cos_sin(turns(m[:8] * STEP)))
-        turn = [tuple(jnp.concatenate([v, v], 0) for v in pair) for pair in turn]
+            here, beside = cos_sin(turns(m * at + shift))
+            rc, rs = (jnp.concatenate([v, v], 0) for v in cos_sin(turns(m[:8] * STEP)))
+            carry.append((here * rc + beside * rs, here))
+            turn.append(rc + rc)
 
         def body(t, state, first=first, turn=turn):
             base = pl.multiple_of(t * STEP, STEP)
             out = []
             for i in range(group):
-                c, s = state[i]
-                rc, rs = turn[i]
+                before, here = state[i]
                 col = (first + i) * LANES
-                tab_ref[pl.ds(base, STEP), col : col + LANES] = c.astype(BF16)
-                out.append((c * rc - s * rs, s * rc + c * rs))
+                tab_ref[pl.ds(base, STEP), col : col + LANES] = here.astype(BF16)
+                out.append((here, turn[i] * here - before))
             return tuple(out)
 
-        lax.fori_loop(0, lons // STEP, body, tuple(carry), unroll=3)
-    copies[1].wait()
-    for d in range(spots):
-        part_ref[SPOTS.index(d)] = jnp.dot(
-            p_ref[...], tab_ref[:, d * LANES : (d + 1) * LANES], preferred_element_type=F32
-        )
+        lax.fori_loop(0, lons // STEP, body, tuple(carry), unroll=5)
+    for d in range(0, spots, 2):
+        pair = jnp.dot(p_ref[...], tab_ref[:, d * LANES : (d + 2) * LANES], preferred_element_type=F32).astype(BF16)
+        part_ref[SPOTS.index(d)] = pair[:, :LANES]
+        part_ref[SPOTS.index(d + 1)] = pair[:, LANES:]
     cycles = cyc.shape[0]
     share = factor_ref.shape[0] // FAR
-    copies[4].wait()
     per = LANES // share
     for far_at in range(FAR):
         lat = lat_index(far_at)
@@ -121,8 +120,6 @@
         factor_ref[far_at * share : (far_at + 1) * share] = DENSITY_RATIO * (
             1.0 + col_ref[far_at, pl.ds(pl.multiple_of(lax.rem(lat, per) * share, share), share), :]
         )
-    copies[2].wait()
-    copies[3].wait()
     sub = iota((cycles, LANES), 0)
     weight = jnp.zeros((cycles, LANES), F32)
     for j in range(cycles):
@@ -135,9 +132,9 @@
     sources, rows, _ = r_ref.shape
     cycles = rows // 2
     half = LANES // 2
-    total = r_ref[0]
+    total = r_ref[0].astype(F32)
     for d in range(1, sources):
-        total = total + r_ref[d]
+        total = total + r_ref[d].astype(F32)
     weight = weight_ref[...]
     lon_scale = 1.0 / math.sqrt(NLON)
     total = total * jnp.where(iota((rows, LANES), 1) < half, lon_scale, -lon_scale)
@@ -238,11 +235,14 @@
         out_ref[d] = signal
 
 
-def inverse_kernel(g_ref, tab_ref, out_ref):
+def inverse_kernel(g_ref, tab_ref, spec_ref, out_ref, spec_hbm, sem):
+    copy = pltpu.make_async_copy(spec_ref, spec_hbm, sem)
+    copy.start()
     spots = g_ref.shape[0]
     lhs = jnp.concatenate([g_ref[SPOTS.index(d)] for d in range(spots)], 1)
     field = lax.dot_general(lhs, tab_ref[...], (((1,), (1,)), ((), ())), preferred_element_type=F32)
     out_ref[...] = field * (1.0 / math.sqrt(spots * (LANES // 2)))
+    copy.wait()
 
 
 VM = pl.BlockSpec(memory_space=pltpu.VMEM)
@@ -261,12 +261,12 @@
     return pltpu.with_memory_space_constraint(x, pltpu.VMEM)
 
 
-def call(kernel, outs, specs, name, mib, flops, scratch=()):
+def call(kernel, outs, specs, name, mib, flops, scratch=(), ends=None):
     return pl.pallas_call(
         kernel,
         out_shape=outs,
         in_specs=specs,
-        out_specs=tuple(VM for _ in outs) if isinstance(outs, tuple) else VM,
+        out_specs=ends or (tuple(VM for _ in outs) if isinstance(outs, tuple) else VM),
         scratch_shapes=list(scratch),
         compiler_params=pltpu.CompilerParams(vmem_limit_bytes=mib << 20),
         cost_estimate=pl.CostEstimate(flops=flops, bytes_accessed=1 << 20, transcendentals=0),
@@ -294,7 +294,7 @@
         forward_kernel,
         (
             shape((lons, n_ord * LANES), BF16),
-            shape((n_ord, rows, LANES), F32),
+            shape((n_ord, rows, LANES), BF16),
             shape((8, LANES), jnp.int32),
             shape((cycles, LANES), F32),
             shape((FAR * share, LANES), F32),
@@ -328,10 +328,10 @@
     sides = swap(coeff.reshape(SIDE, wide, LANES), "x")
     partial = call(side_kernel, shape((FAR, wide, LANES), BF16), [VM], "side", 4, work)(near(sides))
     summands = swap(partial.reshape(FAR * RUN, block, LANES), ("yh", "z"))
-    spectrum, copies = call(
+    own_part, copies = call(
         scale_kernel,
         (
-            jax.ShapeDtypeStruct((2, share, own_orders), F32),
+            shape((2, share, own_orders), F32),
             shape((RUN, block, LANES), BF16),
         ),
         [VM, VM],
@@ -351,9 +351,19 @@
         work,
     )(near(scaled), near(own), near(tab))
     signals = swap(signal, "ord")
-    field = call(inverse_kernel, jax.ShapeDtypeStruct((rows, lons), F32), [VM, VM], "inverse", 6, work)(
-        near(signals), near(table)
-    )
+    field, spectrum = call(
+        inverse_kernel,
+        (
+            jax.ShapeDtypeStruct((rows, lons), F32),
+            pltpu.HBM((2, share, own_orders), F32),
+        ),
+        [VM, VM, VM],
+        "inverse",
+        6,
+        work,
+        [pltpu.SemaphoreType.DMA],
+        (VM, HB),
+    )(near(signals), near(table), near(own_part))
     return jnp.transpose(spectrum, (0, 2, 1)), field.reshape(2, cycles, lons)
 
 

time: 82.3 us -> 81.2 us (0.987)
  Pallas kernels: 5.85 us -> 4.92 us
where the time goes in v4:
time: 81.2 us; the launch traced here: 80.3 us
  blocking collectives  74.7 us (92%)
  Pallas kernels  4.92 us (6%)
    all_to_all x6, blocking collectives, swap(): lax.all_to_all(x, axis, split_axis=0, concat_axis=0, axis_index_groups=[M...  74.7 us
    pallas_call x1, Pallas kernels, per_device(): call(forward_kernel, (shape((lons, n_ord * LANES), BF16), shape((n_ord, r...  1.86 us

profile of v4, /device:TPU:1, one launch (start us, length us, event | category | flops | bytes accessed | tf_op | source)
XLA Modules:
  0.0 80.3 jit_solution(3610702054515826431)
XLA Ops:
  0.6 1.9 %forward.1 = (bf16[720,1024]{1,0:T(8,128)(2,1)S(1)}, bf16[8,16,128]{2,1,0:T(8,128)(2,1)S(1)}, s32[8,128]{1,0:T(8,128)S(1)}, f32[8,128]{1,0:T(8,128)S(1)}, f32[64...) custom-call(s32[4,128]{1,0:T(4,128)} %bitcast.17, bf16[16,720]{1,0:T(8,128)(2,1)} %bitcast.15, s32[8]{0:T(128)} %cyc_hbm.1, ...), custom_call_target="tpu_custom_call" | custom-call | flops 536870912 | bytes 1048576 | tf_op jit(solution)/shard_map/forward/pallas_call | solution.py:293
  2.5 13.5 %all_to_all.30.r_ref = bf16[8,16,128]{2,1,0:T(8,128)(2,1)S(1)} all-to-all(bf16[8,16,128]{2,1,0:T(8,128)(2,1)S(1)} %get-tuple-element.13), channel_id=1, replica_groups={{7,6,5,4,3,2,1,0},{15,14,13,12,11,10,9,8},{23,22,21,20,19,18,17,16},{31..., dimensions={0} | all-to-all | bytes 65536 | tf_op jit(solution)/shard_map/all_to_all | solution.py:278
  16.0 0.8 %analysis.1 = bf16[2048,128]{1,0:T(8,128)(2,1)S(1)} custom-call(f32[8,128]{1,0:T(8,128)S(1)} %get-tuple-element.12.weight_ref, bf16[8,16,128]{2,1,0:T(8,128)(2,1)S(1)} %all_to_all.30.r_ref, s32[8,128]{1,0:T(8,128)S(1)} %get-tuple-element.14.own_ref, bf16[512,2048]{1,0:T(8,128)(2,1)S(1)} %get-tuple-element.15.tab_ref), custom_call_target="tpu_custom_call" | custom-call | flops 536870912 | bytes 1048576 | tf_op jit(solution)/shard_map/analysis/pallas_call | solution.py:318
  16.8 10.2 %all_to_all.31.r_ref = bf16[4,512,128]{2,1,0:T(8,128)(2,1)S(1)} all-to-all(bf16[4,512,128]{2,1,0:T(8,128)(2,1)S(1)} %bitcast.11), channel_id=1, replica_groups={{128,192,0,64},{129,193,1,65},{130,194,2,66},{131,195,3,67},{132,196,4,..., dimensions={0} | all-to-all | bytes 1048576 | tf_op jit(solution)/shard_map/all_to_all | solution.py:278
  27.0 0.1 side.1
  27.1 21.1 %all_to_all.32.r_ref = bf16[16,64,128]{2,1,0:T(8,128)(2,1)S(1)} all-to-all(bf16[16,64,128]{2,1,0:T(8,128)(2,1)S(1)} %bitcast.12), channel_id=1, replica_groups={{288,296,304,312,256,264,272,280,32,40,48,56,0,8,16,24},{289,297,305,31..., dimensions={0} | all-to-all | bytes 524288 | tf_op jit(solution)/shard_map/all_to_all | solution.py:278
  48.2 0.1 scale.1
  48.3 9.5 %all_to_all.33 = bf16[8,64,128]{2,1,0:T(8,128)(2,1)S(1)} all-to-all(bf16[8,64,128]{2,1,0:T(8,128)(2,1)S(1)} %get-tuple-element.17), channel_id=1, replica_groups={{32,40,48,56,0,8,16,24},{33,41,49,57,1,9,17,25},{34,42,50,58,2,10,18,26..., dimensions={0} | all-to-all | bytes 262144 | tf_op jit(solution)/shard_map/all_to_all | solution.py:278
  57.8 0.1 spread.1
  57.9 9.6 %all_to_all.34 = bf16[4,512,128]{2,1,0:T(8,128)(2,1)S(1)} all-to-all(bf16[4,512,128]{2,1,0:T(8,128)(2,1)S(1)} %spread.1), channel_id=1, replica_groups={{128,192,0,64},{129,193,1,65},{130,194,2,66},{131,195,3,67},{132,196,4,..., dimensions={0} | all-to-all | bytes 1048576 | tf_op jit(solution)/shard_map/all_to_all | solution.py:278
  67.5 0.7 synthesis.1
  68.2 10.8 %all_to_all.35.g_ref = bf16[8,16,128]{2,1,0:T(8,128)(2,1)S(1)} all-to-all(bf16[8,16,128]{2,1,0:T(8,128)(2,1)S(1)} %synthesis.1), channel_id=1, replica_groups={{7,6,5,4,3,2,1,0},{15,14,13,12,11,10,9,8},{23,22,21,20,19,18,17,16},{31..., dimensions={0} | all-to-all | bytes 65536 | tf_op jit(solution)/shard_map/all_to_all | solution.py:278
  79.0 1.3 %inverse.1 = (f32[16,720]{1,0:T(8,128)}, f32[2,32,64]{2,1,0:T(8,128)}) custom-call(bf16[8,16,128]{2,1,0:T(8,128)(2,1)S(1)} %all_to_all.35.g_ref, bf16[720,1024]{1,0:T(8,128)(2,1)S(1)} %get-tuple-element.18.tab_ref, f32[2,32,64]{2,1,0:T(8,128)S(1)} %get-tuple-element.19.spec_ref), custom_call_target="tpu_custom_call" | custom-call | flops 536870912 | bytes 1048576 | tf_op jit(solution)/shard_map/inverse/pallas_call | solution.py:354

commit v5 on v4

--- a/solution.py
+++ b/solution.py
@@ -15,12 +15,11 @@
 STEP = 16
 FAR, SIDE, RUN = 2, 4, 8
 LAT = ("yh", "x", "z")
-SIDES = [2, 3, 0, 1]
-RUNS = [4, 5, 6, 7, 0, 1, 2, 3]
-SPOTS = [7, 6, 5, 4, 3, 2, 1, 0]
-MEMBERS = {"x": SIDES, "z": RUNS, "ord": SPOTS, ("yh", "z"): [RUN + z for z in RUNS] + RUNS}
+SIDES, RUNS, SPOTS = [2, 3, 0, 1], [4, 5, 6, 7, 0, 1, 2, 3], [7, 0, 1, 2, 3, 4, 5, 6]
+FARS = [1, 0]
 F32 = jnp.float32
 BF16 = jnp.bfloat16
+SIDES_BACK, RUNS_BACK, SPOTS_BACK = [2, 0, 1, 3], [4, 0, 1, 2, 3, 5, 6, 7], [4, 5, 6, 7, 0, 1, 2, 3]
 
 
 def iota(shape, dim):
@@ -31,9 +30,9 @@
     return (far * SIDE + lax.axis_index("x")) * RUN + lax.axis_index("z")
 
 
-def place(lat):
+def place(lat, sides, runs):
     far, side, run = lat // (SIDE * RUN), lat // RUN % SIDE, lat % RUN
-    return (SIDES.index(side) * RUN + RUNS.index(run)) * FAR + far
+    return (sides.index(side) * RUN + runs.index(run)) * FAR + far
 
 
 def turns(phase):
@@ -107,7 +106,7 @@
 
         lax.fori_loop(0, lons // STEP, body, tuple(carry), unroll=5)
     for d in range(0, spots, 2):
-        pair = jnp.dot(p_ref[...], tab_ref[:, d * LANES : (d + 2) * LANES], preferred_element_type=F32).astype(BF16)
+        pair = jnp.dot(p_ref[...], tab_ref[:, d * LANES : (d + 2) * LANES], preferred_element_type=F32)
         part_ref[SPOTS.index(d)] = pair[:, :LANES]
         part_ref[SPOTS.index(d + 1)] = pair[:, LANES:]
     cycles = cyc.shape[0]
@@ -173,7 +172,7 @@
         for i in range(tile // LANES):
             turned = jnp.transpose(coeff[:, i * LANES : (i + 1) * LANES]).astype(BF16)
             for b in range(LANES // share):
-                at = place((l0 + i * LANES) // share + b) * share
+                at = place((l0 + i * LANES) // share + b, SIDES, RUNS) * share
                 x_ref[at : at + share, :] = turned[b * share : (b + 1) * share]
 
 
@@ -216,7 +215,8 @@
     depth, degrees = tab_ref.shape
     blocks = FAR * SIDE * RUN
     share = degrees // blocks
-    s = jnp.concatenate([s_ref[place(b) * share : (place(b) + 1) * share, :] for b in range(blocks)], 0)
+    starts = [place(b, SIDES_BACK, RUNS_BACK) * share for b in range(blocks)]
+    s = jnp.concatenate([s_ref[at : at + share, :] for at in starts], 0)
     odd_row = (iota((degrees, LANES), 0) & 1) == 1
     flipped = jnp.where(odd_row, -s, s)
     both = jnp.concatenate([s, flipped], 1)
@@ -239,7 +239,7 @@
     copy = pltpu.make_async_copy(spec_ref, spec_hbm, sem)
     copy.start()
     spots = g_ref.shape[0]
-    lhs = jnp.concatenate([g_ref[SPOTS.index(d)] for d in range(spots)], 1)
+    lhs = jnp.concatenate([g_ref[SPOTS_BACK.index(d)] for d in range(spots)], 1)
     field = lax.dot_general(lhs, tab_ref[...], (((1,), (1,)), ((), ())), preferred_element_type=F32)
     out_ref[...] = field * (1.0 / math.sqrt(spots * (LANES // 2)))
     copy.wait()
@@ -274,10 +274,8 @@
     )
 
 
-def swap(x, axis):
-    return lax.all_to_all(
-        x, axis, split_axis=0, concat_axis=0, axis_index_groups=[MEMBERS[axis]], tiled=True
-    )
+def swap(x, axis, members):
+    return lax.all_to_all(x, axis, split_axis=0, concat_axis=0, axis_index_groups=[members], tiled=True)
 
 
 def per_device(pressure, tables, quad_weight, love_number, order_list, cycle_list):
@@ -294,7 +292,7 @@
         forward_kernel,
         (
             shape((lons, n_ord * LANES), BF16),
-            shape((n_ord, rows, LANES), BF16),
+            shape((n_ord, rows, LANES), F32),
             shape((8, LANES), jnp.int32),
             shape((cycles, LANES), F32),
             shape((FAR * share, LANES), F32),
@@ -314,7 +312,7 @@
             pltpu.SemaphoreType.DMA((6,)),
         ],
     )(far(orders), far(pressure.reshape(rows, lons)), far(cycle_list), far(quad_weight), far(love), far(flat))
-    arrived = swap(part, "ord")
+    arrived = swap(part, "ord", SPOTS)
     coeff = call(
         analysis_kernel,
         shape((degrees, LANES), BF16),
@@ -325,9 +323,11 @@
     )(near(weight), near(arrived), near(own), near(tab))
     block = FAR * share
     wide = RUN * block
-    sides = swap(coeff.reshape(SIDE, wide, LANES), "x")
+    sides = swap(coeff.reshape(SIDE, wide, LANES), "x", SIDES)
     partial = call(side_kernel, shape((FAR, wide, LANES), BF16), [VM], "side", 4, work)(near(sides))
-    summands = swap(partial.reshape(FAR * RUN, block, LANES), ("yh", "z"))
+    summands = swap(
+        partial.reshape(FAR * RUN, block, LANES), ("yh", "z"), [far * RUN + z for far in FARS for z in RUNS]
+    )
     own_part, copies = call(
         scale_kernel,
         (
@@ -339,9 +339,9 @@
         4,
         work,
     )(near(summands), near(factor))
-    runs = swap(copies, "z").reshape(wide, LANES)
+    runs = swap(copies, "z", RUNS_BACK).reshape(wide, LANES)
     again = call(spread_kernel, shape((SIDE, wide, LANES), BF16), [VM], "spread", 4, work)(near(runs))
-    scaled = swap(again, "x").reshape(degrees, LANES)
+    scaled = swap(again, "x", SIDES_BACK).reshape(degrees, LANES)
     signal = call(
         synthesis_kernel,
         shape((n_ord, rows, LANES), BF16),
@@ -350,7 +350,7 @@
         8,
         work,
     )(near(scaled), near(own), near(tab))
-    signals = swap(signal, "ord")
+    signals = swap(signal, "ord", SPOTS_BACK)
     field, spectrum = call(
         inverse_kernel,
         (

time: 81.2 us -> 79.9 us (0.984)
  blocking collectives: 74.7 us -> 73.5 us
    all_to_all x6, blocking collectives: 74.7 us -> 73.5 us  [swap(): lax.all_to_all(x, axis, split_axis=0, concat_axis=0, axis_index_groups=[m...]
where the time goes in v5:
time: 79.9 us; the launch traced here: 79.1 us
  blocking collectives  73.5 us (92%)
  Pallas kernels  4.92 us (6%)
    all_to_all x6, blocking collectives, swap(): lax.all_to_all(x, axis, split_axis=0, concat_axis=0, axis_index_groups=[m...  73.5 us
    pallas_call x1, Pallas kernels, per_device(): call(forward_kernel, (shape((lons, n_ord * LANES), BF16), shape((n_ord, r...  1.86 us

profile of v5, /device:TPU:1, one launch (start us, length us, event | category | flops | bytes accessed | tf_op | source)
XLA Modules:
  0.0 79.1 jit_solution(12115957302668479152)
XLA Ops:
  0.6 1.9 %forward.1 = (bf16[720,1024]{1,0:T(8,128)(2,1)S(1)}, f32[8,16,128]{2,1,0:T(8,128)S(1)}, s32[8,128]{1,0:T(8,128)S(1)}, f32[8,128]{1,0:T(8,128)S(1)}, f32[64,128]{...) custom-call(s32[4,128]{1,0:T(4,128)} %bitcast.17, bf16[16,720]{1,0:T(8,128)(2,1)} %bitcast.15, s32[8]{0:T(128)} %cyc_hbm.1, ...), custom_call_target="tpu_custom_call" | custom-call | flops 536870912 | bytes 1048576 | tf_op jit(solution)/shard_map/forward/pallas_call | solution.py:291
  2.5 13.6 %all_to_all.30.r_ref = f32[8,16,128]{2,1,0:T(8,128)S(1)} all-to-all(f32[8,16,128]{2,1,0:T(8,128)S(1)} %get-tuple-element.13), channel_id=1, replica_groups={{7,0,1,2,3,4,5,6},{15,8,9,10,11,12,13,14},{23,16,17,18,19,20,21,22},{31..., dimensions={0} | all-to-all | bytes 131072 | tf_op jit(solution)/shard_map/all_to_all | solution.py:278
  16.1 0.8 %analysis.1 = bf16[2048,128]{1,0:T(8,128)(2,1)S(1)} custom-call(f32[8,128]{1,0:T(8,128)S(1)} %get-tuple-element.12.weight_ref, f32[8,16,128]{2,1,0:T(8,128)S(1)} %all_to_all.30.r_ref, s32[8,128]{1,0:T(8,128)S(1)} %get-tuple-element.14.own_ref, bf16[512,2048]{1,0:T(8,128)(2,1)S(1)} %get-tuple-element.15.tab_ref), custom_call_target="tpu_custom_call" | custom-call | flops 536870912 | bytes 1048576 | tf_op jit(solution)/shard_map/analysis/pallas_call | solution.py:316
  17.0 9.9 %all_to_all.31.r_ref = bf16[4,512,128]{2,1,0:T(8,128)(2,1)S(1)} all-to-all(bf16[4,512,128]{2,1,0:T(8,128)(2,1)S(1)} %bitcast.11), channel_id=1, replica_groups={{128,192,0,64},{129,193,1,65},{130,194,2,66},{131,195,3,67},{132,196,4,..., dimensions={0} | all-to-all | bytes 1048576 | tf_op jit(solution)/shard_map/all_to_all | solution.py:278
  26.8 0.1 side.1
  26.9 21.4 %all_to_all.32.r_ref = bf16[16,64,128]{2,1,0:T(8,128)(2,1)S(1)} all-to-all(bf16[16,64,128]{2,1,0:T(8,128)(2,1)S(1)} %bitcast.12), channel_id=1, replica_groups={{288,296,304,312,256,264,272,280,32,40,48,56,0,8,16,24},{289,297,305,31..., dimensions={0} | all-to-all | bytes 524288 | tf_op jit(solution)/shard_map/all_to_all | solution.py:278
  48.3 0.1 scale.1
  48.4 9.2 %all_to_all.33 = bf16[8,64,128]{2,1,0:T(8,128)(2,1)S(1)} all-to-all(bf16[8,64,128]{2,1,0:T(8,128)(2,1)S(1)} %get-tuple-element.17), channel_id=1, replica_groups={{32,0,8,16,24,40,48,56},{33,1,9,17,25,41,49,57},{34,2,10,18,26,42,50,58..., dimensions={0} | all-to-all | bytes 262144 | tf_op jit(solution)/shard_map/all_to_all | solution.py:278
  57.6 0.1 spread.1
  57.7 9.4 %all_to_all.34 = bf16[4,512,128]{2,1,0:T(8,128)(2,1)S(1)} all-to-all(bf16[4,512,128]{2,1,0:T(8,128)(2,1)S(1)} %spread.1), channel_id=1, replica_groups={{128,0,64,192},{129,1,65,193},{130,2,66,194},{131,3,67,195},{132,4,68,1..., dimensions={0} | all-to-all | bytes 1048576 | tf_op jit(solution)/shard_map/all_to_all | solution.py:278
  67.1 0.7 synthesis.1
  67.8 10.0 %all_to_all.35.g_ref = bf16[8,16,128]{2,1,0:T(8,128)(2,1)S(1)} all-to-all(bf16[8,16,128]{2,1,0:T(8,128)(2,1)S(1)} %synthesis.1), channel_id=1, replica_groups={{4,5,6,7,0,1,2,3},{12,13,14,15,8,9,10,11},{20,21,22,23,16,17,18,19},{28..., dimensions={0} | all-to-all | bytes 65536 | tf_op jit(solution)/shard_map/all_to_all | solution.py:278
  77.8 1.3 %inverse.1 = (f32[16,720]{1,0:T(8,128)}, f32[2,32,64]{2,1,0:T(8,128)}) custom-call(bf16[8,16,128]{2,1,0:T(8,128)(2,1)S(1)} %all_to_all.35.g_ref, bf16[720,1024]{1,0:T(8,128)(2,1)S(1)} %get-tuple-element.18.tab_ref, f32[2,32,64]{2,1,0:T(8,128)S(1)} %get-tuple-element.19.spec_ref), custom_call_target="tpu_custom_call" | custom-call | flops 536870912 | bytes 1048576 | tf_op jit(solution)/shard_map/inverse/pallas_call | solution.py:354

commit v6 on v5

--- a/solution.py
+++ b/solution.py
@@ -15,7 +15,7 @@
 STEP = 16
 FAR, SIDE, RUN = 2, 4, 8
 LAT = ("yh", "x", "z")
-SIDES, RUNS, SPOTS = [2, 3, 0, 1], [4, 5, 6, 7, 0, 1, 2, 3], [7, 0, 1, 2, 3, 4, 5, 6]
+SIDES, RUNS, SPOTS = [2, 3, 0, 1], [6, 7, 5, 4, 0, 1, 2, 3], [7, 0, 1, 2, 3, 4, 5, 6]
 FARS = [1, 0]
 F32 = jnp.float32
 BF16 = jnp.bfloat16
@@ -83,32 +83,30 @@
     for copy in copies[:5]:
         copy.wait()
     own_ref[...] = order_rows(o_ref, lax.axis_index("ord"), own_ref.shape[0])
-    group = 4
-    for first in range(0, spots, group):
-        carry = []
-        turn = []
-        for d in range(first, first + group):
-            m = order_rows(o_ref, d, STEP).astype(F32)
-            here, beside = cos_sin(turns(m * at + shift))
-            rc, rs = (jnp.concatenate([v, v], 0) for v in cos_sin(turns(m[:8] * STEP)))
-            carry.append((here * rc + beside * rs, here))
-            turn.append(rc + rc)
-
-        def body(t, state, first=first, turn=turn):
-            base = pl.multiple_of(t * STEP, STEP)
-            out = []
-            for i in range(group):
-                before, here = state[i]
-                col = (first + i) * LANES
-                tab_ref[pl.ds(base, STEP), col : col + LANES] = here.astype(BF16)
-                out.append((here, turn[i] * here - before))
-            return tuple(out)
-
-        lax.fori_loop(0, lons // STEP, body, tuple(carry), unroll=5)
-    for d in range(0, spots, 2):
-        pair = jnp.dot(p_ref[...], tab_ref[:, d * LANES : (d + 2) * LANES], preferred_element_type=F32)
-        part_ref[SPOTS.index(d)] = pair[:, :LANES]
-        part_ref[SPOTS.index(d + 1)] = pair[:, LANES:]
+    state, turn = [], []
+    for d in range(spots):
+        m = order_rows(o_ref, d, STEP).astype(F32)
+        here, beside = cos_sin(turns(m * at + shift))
+        rc, rs = (jnp.concatenate([v, v], 0) for v in cos_sin(turns(m[:8] * STEP)))
+        state.append((here * rc + beside * rs, here))
+        turn.append(rc + rc)
+    sums = [None] * (spots // 2)
+    deep = 2 * LANES
+    for top in range(0, lons, deep):
+        end = min(top + deep, lons)
+        for base in range(top, end, STEP):
+            for d in range(spots):
+                before, here = state[d]
+                tab_ref[base : base + STEP, d * LANES : (d + 1) * LANES] = here.astype(BF16)
+                state[d] = (here, turn[d] * here - before)
+        for i in range(spots // 2):
+            term = jnp.dot(
+                p_ref[:, top:end], tab_ref[top:end, 2 * i * LANES : 2 * (i + 1) * LANES], preferred_element_type=F32
+            )
+            sums[i] = term if sums[i] is None else sums[i] + term
+    for d in range(spots):
+        half = d % 2 * LANES
+        part_ref[SPOTS.index(d)] = sums[d // 2][:, half : half + LANES]
     cycles = cyc.shape[0]
     share = factor_ref.shape[0] // FAR
     per = LANES // share
@@ -170,7 +168,7 @@
         coeff = jnp.where(((degree + order) & 1) == 0, even, odd)
         coeff = jnp.where(degree >= order, coeff, 0.0)
         for i in range(tile // LANES):
-            turned = jnp.transpose(coeff[:, i * LANES : (i + 1) * LANES]).astype(BF16)
+            turned = jnp.transpose(coeff[:, i * LANES : (i + 1) * LANES].astype(BF16))
             for b in range(LANES // share):
                 at = place((l0 + i * LANES) // share + b, SIDES, RUNS) * share
                 x_ref[at : at + share, :] = turned[b * share : (b + 1) * share]
@@ -235,14 +233,20 @@
         out_ref[d] = signal
 
 
-def inverse_kernel(g_ref, tab_ref, spec_ref, out_ref, spec_hbm, sem):
-    copy = pltpu.make_async_copy(spec_ref, spec_hbm, sem)
-    copy.start()
+def inverse_kernel(g_ref, tab_ref, spec_ref, field_hbm, spec_hbm, out_ref, sems):
+    copies = [pltpu.make_async_copy(spec_ref, spec_hbm, sems.at[0])]
+    copies[0].start()
     spots = g_ref.shape[0]
+    lons = out_ref.shape[1]
     lhs = jnp.concatenate([g_ref[SPOTS_BACK.index(d)] for d in range(spots)], 1)
-    field = lax.dot_general(lhs, tab_ref[...], (((1,), (1,)), ((), ())), preferred_element_type=F32)
-    out_ref[...] = field * (1.0 / math.sqrt(spots * (LANES // 2)))
-    copy.wait()
+    cut = 4 * LANES
+    for i, (low, high) in enumerate(((0, cut), (cut, lons))):
+        part = lax.dot_general(lhs, tab_ref[low:high, :], (((1,), (1,)), ((), ())), preferred_element_type=F32)
+        out_ref[:, low:high] = part * (1.0 / math.sqrt(spots * (LANES // 2)))
+        copies.append(pltpu.make_async_copy(out_ref.at[:, low:high], field_hbm.at[:, low:high], sems.at[i + 1]))
+        copies[-1].start()
+    for copy in copies:
+        copy.wait()
 
 
 VM = pl.BlockSpec(memory_space=pltpu.VMEM)
@@ -354,15 +358,15 @@
     field, spectrum = call(
         inverse_kernel,
         (
-            jax.ShapeDtypeStruct((rows, lons), F32),
+            pltpu.HBM((rows, lons), F32),
             pltpu.HBM((2, share, own_orders), F32),
         ),
         [VM, VM, VM],
         "inverse",
         6,
         work,
-        [pltpu.SemaphoreType.DMA],
-        (VM, HB),
+        [pltpu.VMEM((rows, lons), F32), pltpu.SemaphoreType.DMA((3,))],
+        (HB, HB),
     )(near(signals), near(table), near(own_part))
     return jnp.transpose(spectrum, (0, 2, 1)), field.reshape(2, cycles, lons)
 

time: 79.9 us -> 79.6 us (level)
  no operation moved by 1% of the time
where the time goes in v6:
time: 79.6 us; the launch traced here: 78.8 us
  blocking collectives  73.5 us (92%)
  Pallas kernels  4.66 us (6%)
    all_to_all x6, blocking collectives, swap(): lax.all_to_all(x, axis, split_axis=0, concat_axis=0, axis_index_groups=[m...  73.5 us
    pallas_call x1, Pallas kernels, per_device(): call(forward_kernel, (shape((lons, n_ord * LANES), BF16), shape((n_ord, r...  1.76 us

profile of v6, /device:TPU:1, one launch (start us, length us, event | category | flops | bytes accessed | tf_op | source)
XLA Modules:
  0.0 78.8 jit_solution(6293233791928181344)
XLA Ops:
  0.6 1.8 %forward.1 = (bf16[720,1024]{1,0:T(8,128)(2,1)S(1)}, f32[8,16,128]{2,1,0:T(8,128)S(1)}, s32[8,128]{1,0:T(8,128)S(1)}, f32[8,128]{1,0:T(8,128)S(1)}, f32[64,128]{...) custom-call(s32[4,128]{1,0:T(4,128)} %bitcast.17, bf16[16,720]{1,0:T(8,128)(2,1)} %bitcast.15, s32[8]{0:T(128)} %cyc_hbm.1, ...), custom_call_target="tpu_custom_call" | custom-call | flops 536870912 | bytes 1048576 | tf_op jit(solution)/shard_map/forward/pallas_call | solution.py:295
  2.4 13.6 %all_to_all.30.r_ref = f32[8,16,128]{2,1,0:T(8,128)S(1)} all-to-all(f32[8,16,128]{2,1,0:T(8,128)S(1)} %get-tuple-element.13), channel_id=1, replica_groups={{7,0,1,2,3,4,5,6},{15,8,9,10,11,12,13,14},{23,16,17,18,19,20,21,22},{31..., dimensions={0} | all-to-all | bytes 131072 | tf_op jit(solution)/shard_map/all_to_all | solution.py:282
  16.0 0.8 analysis.1
  16.8 9.9 %all_to_all.31.r_ref = bf16[4,512,128]{2,1,0:T(8,128)(2,1)S(1)} all-to-all(bf16[4,512,128]{2,1,0:T(8,128)(2,1)S(1)} %bitcast.11), channel_id=1, replica_groups={{128,192,0,64},{129,193,1,65},{130,194,2,66},{131,195,3,67},{132,196,4,..., dimensions={0} | all-to-all | bytes 1048576 | tf_op jit(solution)/shard_map/all_to_all | solution.py:282
  26.7 0.1 side.1
  26.8 18.5 %all_to_all.32.r_ref = bf16[16,64,128]{2,1,0:T(8,128)(2,1)S(1)} all-to-all(bf16[16,64,128]{2,1,0:T(8,128)(2,1)S(1)} %bitcast.12), channel_id=1, replica_groups={{304,312,296,288,256,264,272,280,48,56,40,32,0,8,16,24},{305,313,297,28..., dimensions={0} | all-to-all | bytes 524288 | tf_op jit(solution)/shard_map/all_to_all | solution.py:282
  45.3 0.1 scale.1
  45.4 10.7 %all_to_all.33 = bf16[8,64,128]{2,1,0:T(8,128)(2,1)S(1)} all-to-all(bf16[8,64,128]{2,1,0:T(8,128)(2,1)S(1)} %get-tuple-element.17), channel_id=1, replica_groups={{32,0,8,16,24,40,48,56},{33,1,9,17,25,41,49,57},{34,2,10,18,26,42,50,58..., dimensions={0} | all-to-all | bytes 262144 | tf_op jit(solution)/shard_map/all_to_all | solution.py:282
  56.1 0.1 spread.1
  56.1 8.8 %all_to_all.34 = bf16[4,512,128]{2,1,0:T(8,128)(2,1)S(1)} all-to-all(bf16[4,512,128]{2,1,0:T(8,128)(2,1)S(1)} %spread.1), channel_id=1, replica_groups={{128,0,64,192},{129,1,65,193},{130,2,66,194},{131,3,67,195},{132,4,68,1..., dimensions={0} | all-to-all | bytes 1048576 | tf_op jit(solution)/shard_map/all_to_all | solution.py:282
  65.0 0.7 synthesis.1
  65.7 12.0 %all_to_all.35.g_ref = bf16[8,16,128]{2,1,0:T(8,128)(2,1)S(1)} all-to-all(bf16[8,16,128]{2,1,0:T(8,128)(2,1)S(1)} %synthesis.1), channel_id=1, replica_groups={{4,5,6,7,0,1,2,3},{12,13,14,15,8,9,10,11},{20,21,22,23,16,17,18,19},{28..., dimensions={0} | all-to-all | bytes 65536 | tf_op jit(solution)/shard_map/all_to_all | solution.py:282
  77.7 1.1 %inverse.1 = (f32[16,720]{1,0:T(8,128)}, f32[2,32,64]{2,1,0:T(8,128)}) custom-call(bf16[8,16,128]{2,1,0:T(8,128)(2,1)S(1)} %all_to_all.35.g_ref, bf16[720,1024]{1,0:T(8,128)(2,1)S(1)} %get-tuple-element.18.tab_ref, f32[2,32,64]{2,1,0:T(8,128)S(1)} %get-tuple-element.19.spec_ref), custom_call_target="tpu_custom_call" | custom-call | flops 536870912 | bytes 1048576 | tf_op jit(solution)/shard_map/inverse/pallas_call | solution.py:358

commit v7 on v6

--- a/solution.py
+++ b/solution.py
@@ -214,11 +214,15 @@
     blocks = FAR * SIDE * RUN
     share = degrees // blocks
     starts = [place(b, SIDES_BACK, RUNS_BACK) * share for b in range(blocks)]
-    s = jnp.concatenate([s_ref[at : at + share, :] for at in starts], 0)
-    odd_row = (iota((degrees, LANES), 0) & 1) == 1
-    flipped = jnp.where(odd_row, -s, s)
-    both = jnp.concatenate([s, flipped], 1)
-    result = jnp.dot(tab_ref[...], both, preferred_element_type=F32)
+    deep = 2 * LANES
+    odd_row = (iota((deep, LANES), 0) & 1) == 1
+    result = None
+    for top in range(0, degrees, deep):
+        held = starts[top // share : (top + deep) // share]
+        s = jnp.concatenate([s_ref[at : at + share, :] for at in held], 0)
+        both = jnp.concatenate([s, jnp.where(odd_row, -s, s)], 1)
+        term = jnp.dot(tab_ref[:, top : top + deep], both, preferred_element_type=F32)
+        result = term if result is None else result + term
     lane = lax.rem(iota((cycles, 2 * LANES), 1), half)
     picked = jnp.zeros((cycles, 2 * LANES), F32)
     for m in range(half):

time: 79.6 us -> 79.5 us (level)
  no operation moved by 1% of the time
where the time goes in v7:
time: 79.5 us; the launch traced here: 78.8 us
  blocking collectives  73.5 us (92%)
  Pallas kernels  4.64 us (6%)
    all_to_all x6, blocking collectives, swap(): lax.all_to_all(x, axis, split_axis=0, concat_axis=0, axis_index_groups=[m...  73.5 us
    pallas_call x1, Pallas kernels, per_device(): call(forward_kernel, (shape((lons, n_ord * LANES), BF16), shape((n_ord, r...  1.76 us

profile of v7, /device:TPU:1, one launch (start us, length us, event | category | flops | bytes accessed | tf_op | source)
XLA Modules:
  0.0 78.8 jit_solution(9371164121005482802)
XLA Ops:
  0.6 1.8 %forward.1 = (bf16[720,1024]{1,0:T(8,128)(2,1)S(1)}, f32[8,16,128]{2,1,0:T(8,128)S(1)}, s32[8,128]{1,0:T(8,128)S(1)}, f32[8,128]{1,0:T(8,128)S(1)}, f32[64,128]{...) custom-call(s32[4,128]{1,0:T(4,128)} %bitcast.17, bf16[16,720]{1,0:T(8,128)(2,1)} %bitcast.15, s32[8]{0:T(128)} %cyc_hbm.1, ...), custom_call_target="tpu_custom_call" | custom-call | flops 536870912 | bytes 1048576 | tf_op jit(solution)/shard_map/forward/pallas_call | solution.py:299
  2.4 13.6 %all_to_all.30.r_ref = f32[8,16,128]{2,1,0:T(8,128)S(1)} all-to-all(f32[8,16,128]{2,1,0:T(8,128)S(1)} %get-tuple-element.13), channel_id=1, replica_groups={{7,0,1,2,3,4,5,6},{15,8,9,10,11,12,13,14},{23,16,17,18,19,20,21,22},{31..., dimensions={0} | all-to-all | bytes 131072 | tf_op jit(solution)/shard_map/all_to_all | solution.py:286
  16.0 0.8 analysis.1
  16.8 9.9 %all_to_all.31.r_ref = bf16[4,512,128]{2,1,0:T(8,128)(2,1)S(1)} all-to-all(bf16[4,512,128]{2,1,0:T(8,128)(2,1)S(1)} %bitcast.11), channel_id=1, replica_groups={{128,192,0,64},{129,193,1,65},{130,194,2,66},{131,195,3,67},{132,196,4,..., dimensions={0} | all-to-all | bytes 1048576 | tf_op jit(solution)/shard_map/all_to_all | solution.py:286
  26.7 0.1 side.1
  26.8 18.5 %all_to_all.32.r_ref = bf16[16,64,128]{2,1,0:T(8,128)(2,1)S(1)} all-to-all(bf16[16,64,128]{2,1,0:T(8,128)(2,1)S(1)} %bitcast.12), channel_id=1, replica_groups={{304,312,296,288,256,264,272,280,48,56,40,32,0,8,16,24},{305,313,297,28..., dimensions={0} | all-to-all | bytes 524288 | tf_op jit(solution)/shard_map/all_to_all | solution.py:286
  45.3 0.1 scale.1
  45.4 10.7 %all_to_all.33 = bf16[8,64,128]{2,1,0:T(8,128)(2,1)S(1)} all-to-all(bf16[8,64,128]{2,1,0:T(8,128)(2,1)S(1)} %get-tuple-element.17), channel_id=1, replica_groups={{32,0,8,16,24,40,48,56},{33,1,9,17,25,41,49,57},{34,2,10,18,26,42,50,58..., dimensions={0} | all-to-all | bytes 262144 | tf_op jit(solution)/shard_map/all_to_all | solution.py:286
  56.1 0.1 spread.1
  56.1 8.8 %all_to_all.34 = bf16[4,512,128]{2,1,0:T(8,128)(2,1)S(1)} all-to-all(bf16[4,512,128]{2,1,0:T(8,128)(2,1)S(1)} %spread.1), channel_id=1, replica_groups={{128,0,64,192},{129,1,65,193},{130,2,66,194},{131,3,67,195},{132,4,68,1..., dimensions={0} | all-to-all | bytes 1048576 | tf_op jit(solution)/shard_map/all_to_all | solution.py:286
  65.0 0.7 synthesis.1
  65.7 12.0 %all_to_all.35.g_ref = bf16[8,16,128]{2,1,0:T(8,128)(2,1)S(1)} all-to-all(bf16[8,16,128]{2,1,0:T(8,128)(2,1)S(1)} %synthesis.1), channel_id=1, replica_groups={{4,5,6,7,0,1,2,3},{12,13,14,15,8,9,10,11},{20,21,22,23,16,17,18,19},{28..., dimensions={0} | all-to-all | bytes 65536 | tf_op jit(solution)/shard_map/all_to_all | solution.py:286
  77.7 1.1 %inverse.1 = (f32[16,720]{1,0:T(8,128)}, f32[2,32,64]{2,1,0:T(8,128)}) custom-call(bf16[8,16,128]{2,1,0:T(8,128)(2,1)S(1)} %all_to_all.35.g_ref, bf16[720,1024]{1,0:T(8,128)(2,1)S(1)} %get-tuple-element.18.tab_ref, f32[2,32,64]{2,1,0:T(8,128)S(1)} %get-tuple-element.19.spec_ref), custom_call_target="tpu_custom_call" | custom-call | flops 536870912 | bytes 1048576 | tf_op jit(solution)/shard_map/inverse/pallas_call | solution.py:362

commit v8 on v7

--- a/solution.py
+++ b/solution.py
@@ -19,7 +19,7 @@
 FARS = [1, 0]
 F32 = jnp.float32
 BF16 = jnp.bfloat16
-SIDES_BACK, RUNS_BACK, SPOTS_BACK = [2, 0, 1, 3], [4, 0, 1, 2, 3, 5, 6, 7], [4, 5, 6, 7, 0, 1, 2, 3]
+SIDES_BACK, RUNS_BACK, SPOTS_BACK = [2, 0, 1, 3], [4, 0, 1, 2, 3, 5, 6, 7], [4, 6, 7, 0, 1, 2, 3, 5]
 
 
 def iota(shape, dim):

time: 79.5 us -> 79.5 us (level)
  no operation moved by 1% of the time
where the time goes in v8:
time: 79.5 us; the launch traced here: 78.8 us
  blocking collectives  73.5 us (92%)
  Pallas kernels  4.64 us (6%)
    all_to_all x6, blocking collectives, swap(): lax.all_to_all(x, axis, split_axis=0, concat_axis=0, axis_index_groups=[m...  73.5 us
    pallas_call x1, Pallas kernels, per_device(): call(forward_kernel, (shape((lons, n_ord * LANES), BF16), shape((n_ord, r...  1.76 us

profile of v8, /device:TPU:1, one launch (start us, length us, event | category | flops | bytes accessed | tf_op | source)
XLA Modules:
  0.0 78.8 jit_solution(9028349883587577603)
XLA Ops:
  0.6 1.8 %forward.1 = (bf16[720,1024]{1,0:T(8,128)(2,1)S(1)}, f32[8,16,128]{2,1,0:T(8,128)S(1)}, s32[8,128]{1,0:T(8,128)S(1)}, f32[8,128]{1,0:T(8,128)S(1)}, f32[64,128]{...) custom-call(s32[4,128]{1,0:T(4,128)} %bitcast.17, bf16[16,720]{1,0:T(8,128)(2,1)} %bitcast.15, s32[8]{0:T(128)} %cyc_hbm.1, ...), custom_call_target="tpu_custom_call" | custom-call | flops 536870912 | bytes 1048576 | tf_op jit(solution)/shard_map/forward/pallas_call | solution.py:299
  2.4 13.6 %all_to_all.30.r_ref = f32[8,16,128]{2,1,0:T(8,128)S(1)} all-to-all(f32[8,16,128]{2,1,0:T(8,128)S(1)} %get-tuple-element.13), channel_id=1, replica_groups={{7,0,1,2,3,4,5,6},{15,8,9,10,11,12,13,14},{23,16,17,18,19,20,21,22},{31..., dimensions={0} | all-to-all | bytes 131072 | tf_op jit(solution)/shard_map/all_to_all | solution.py:286
  16.0 0.8 analysis.1
  16.8 9.9 %all_to_all.31.r_ref = bf16[4,512,128]{2,1,0:T(8,128)(2,1)S(1)} all-to-all(bf16[4,512,128]{2,1,0:T(8,128)(2,1)S(1)} %bitcast.11), channel_id=1, replica_groups={{128,192,0,64},{129,193,1,65},{130,194,2,66},{131,195,3,67},{132,196,4,..., dimensions={0} | all-to-all | bytes 1048576 | tf_op jit(solution)/shard_map/all_to_all | solution.py:286
  26.7 0.1 side.1
  26.8 18.5 %all_to_all.32.r_ref = bf16[16,64,128]{2,1,0:T(8,128)(2,1)S(1)} all-to-all(bf16[16,64,128]{2,1,0:T(8,128)(2,1)S(1)} %bitcast.12), channel_id=1, replica_groups={{304,312,296,288,256,264,272,280,48,56,40,32,0,8,16,24},{305,313,297,28..., dimensions={0} | all-to-all | bytes 524288 | tf_op jit(solution)/shard_map/all_to_all | solution.py:286
  45.3 0.1 scale.1
  45.4 10.7 %all_to_all.33 = bf16[8,64,128]{2,1,0:T(8,128)(2,1)S(1)} all-to-all(bf16[8,64,128]{2,1,0:T(8,128)(2,1)S(1)} %get-tuple-element.17), channel_id=1, replica_groups={{32,0,8,16,24,40,48,56},{33,1,9,17,25,41,49,57},{34,2,10,18,26,42,50,58..., dimensions={0} | all-to-all | bytes 262144 | tf_op jit(solution)/shard_map/all_to_all | solution.py:286
  56.1 0.1 spread.1
  56.1 8.8 %all_to_all.34 = bf16[4,512,128]{2,1,0:T(8,128)(2,1)S(1)} all-to-all(bf16[4,512,128]{2,1,0:T(8,128)(2,1)S(1)} %spread.1), channel_id=1, replica_groups={{128,0,64,192},{129,1,65,193},{130,2,66,194},{131,3,67,195},{132,4,68,1..., dimensions={0} | all-to-all | bytes 1048576 | tf_op jit(solution)/shard_map/all_to_all | solution.py:286
  65.0 0.7 synthesis.1
  65.7 12.0 %all_to_all.35.g_ref = bf16[8,16,128]{2,1,0:T(8,128)(2,1)S(1)} all-to-all(bf16[8,16,128]{2,1,0:T(8,128)(2,1)S(1)} %synthesis.1), channel_id=1, replica_groups={{4,6,7,0,1,2,3,5},{12,14,15,8,9,10,11,13},{20,22,23,16,17,18,19,21},{28..., dimensions={0} | all-to-all | bytes 65536 | tf_op jit(solution)/shard_map/all_to_all | solution.py:286
  77.7 1.1 %inverse.1 = (f32[16,720]{1,0:T(8,128)}, f32[2,32,64]{2,1,0:T(8,128)}) custom-call(bf16[8,16,128]{2,1,0:T(8,128)(2,1)S(1)} %all_to_all.35.g_ref, bf16[720,1024]{1,0:T(8,128)(2,1)S(1)} %get-tuple-element.18.tab_ref, f32[2,32,64]{2,1,0:T(8,128)S(1)} %get-tuple-element.19.spec_ref), custom_call_target="tpu_custom_call" | custom-call | flops 536870912 | bytes 1048576 | tf_op jit(solution)/shard_map/inverse/pallas_call | solution.py:362
